TPU v7x, 128 devices: a whole 4x4x4 slice. The times are simulated.
128 devices in a mesh: pair: 64 (over x, y, z), rep: 2 (over core).
Axes of the slice: x: 4, y: 4, z: 4, core: 2. Of those that a mesh axis runs over, the one named last changes fastest.
Arguments:
- triplet_pairs: int32 [1024, 3], P(('pair', 'rep')), may hold values from 0 to 4095, as said below
- tno_width: int32 [1024], P(('pair', 'rep')), may hold values from 64 to 128
- pair_width: int32 [4096], P('pair'), may hold values from 32 to 64
- pair_coeff: bfloat16 [4096, 64, 1024], P('pair'), may hold values from -0.1875 to 0.1875
- pair_amps: bfloat16 [4096, 64, 64], P('pair'), may hold values from -0.03125 to 0.03125
- pair_exch: bfloat16 [4096, 64, 64], P('pair'), may hold values from -0.3125 to 0.3125
- tno_coeff: bfloat16 [1024, 1024, 128], P(('pair', 'rep')), may hold values from -0.1875 to 0.1875
- int_left: bfloat16 [1024, 3, 128, 128], P(('pair', 'rep')), may hold values from -6 to 6
- int_right: bfloat16 [1024, 3, 128, 128], P(('pair', 'rep')), may hold values from -6 to 6
- singles: float32 [1024, 3, 128], P(('pair', 'rep')), may hold values from -6 to 6
- tno_energy: float32 [1024, 128], P(('pair', 'rep')), may hold values from 0.5 to 5
- gap: float32 [1024], P(('pair', 'rep')), may hold values from 1 to 4
Outputs:
- triplet_energy: float32 [1024], P(('pair', 'rep'))
- pair_energy: float32 [4096], P('pair')
Inputs may be any that keep to these rules, and one draw needn't show every extreme that they name: `triplet_pairs`: pair p is owned by index p // 64 of axis pair. The triplets of one chip are rows 2 * c * 8 to 2 * (c + 1) * 8 - 1; among their 48 pair ids at most 1 have one owner, and in every chip some owner has exactly 1 of them.
All inputs are finite; a program needn't handle non-finite values.
Results may differ from a plain program's by a relative error of at most 0.00044.
Values may be sent and summed in bfloat16 or wider, within the bound.
No kernel may reach another device: no remote copies, remote signals or barrier semaphores. Data moves between devices by JAX's collectives and lax.ppermute only.
A program may use at most 128 MiB of HBM per device.

v0:
```python
import jax
import jax.numpy as jnp
from jax import lax
from jax.sharding import PartitionSpec as P


def joined_along(parts, dim):
    lengths = list(parts.shape[1:])
    lengths[dim] *= parts.shape[0]
    return jnp.moveaxis(parts, 0, dim).reshape(lengths)


def sent_to_all(x, axis):
    copies = jnp.broadcast_to(x, (lax.axis_size(axis), *x.shape))
    return lax.all_to_all(copies, axis, split_axis=0, concat_axis=0, tiled=True)


def gathered_copies(x, axis, dim):
    return joined_along(sent_to_all(x, axis), dim)


def in_one_piece(arrays, axis, split_dim, concat_dim, along):
    widths = [a.shape[along] for a in arrays]
    both = jnp.concatenate(arrays, axis=along)
    out = lax.all_to_all(both, axis, split_axis=split_dim, concat_axis=concat_dim, tiled=True)
    return tuple(jnp.split(out, [sum(widths[:k]) for k in range(1, len(widths))], axis=along))


def cut_along(x, dim, size):
    lengths = x.shape
    parts = x.reshape(*lengths[:dim], size, lengths[dim] // size, *lengths[dim + 1 :])
    return jnp.moveaxis(parts, dim, 0)


def sum_at_owner(x, axis, dim):
    size = lax.axis_size(axis)
    parts = lax.all_to_all(cut_along(x, dim, size), axis, 0, 0, tiled=True)
    return jnp.sum(parts, axis=0)


def gathered_total(x, axis):
    return lax.all_gather(x, axis).sum(0)


def projected_energy(
    pno_coeff, pno_blocks, tno_block, tno_count, left, right, single_amps, tno_levels, shift
):
    tno_size = tno_block.shape[1]
    pno_size = pno_coeff.shape[1]
    kept_cols = (jnp.arange(tno_size, dtype=jnp.int32) < tno_count).astype(jnp.float32)
    tno_kept = tno_block * kept_cols.astype(jnp.bfloat16)[None, :]
    intersection = jnp.einsum(
        "xad,db->xab", pno_coeff, tno_kept, preferred_element_type=jnp.float32
    ).astype(jnp.bfloat16)
    halfway = jnp.einsum(
        "xab,xac->xbc", intersection, pno_blocks, preferred_element_type=jnp.float32
    ).astype(jnp.bfloat16)
    halfway = halfway.reshape(3, tno_size, 2, pno_size)
    projected = jnp.einsum(
        "xbkc,xcd->xkbd", halfway, intersection, preferred_element_type=jnp.float32
    )
    amps_tno = projected[:, 0].astype(jnp.bfloat16)
    exch_tno = projected[:, 1]
    left_cols = jnp.transpose(left, (2, 0, 1)).reshape(tno_size, 3 * tno_size)
    right_cols = jnp.transpose(right, (2, 0, 1)).reshape(tno_size, 3 * tno_size)
    khatri = (left_cols[:, None, :] * right_cols[None, :, :]).reshape(
        tno_size * tno_size, 3 * tno_size
    )
    leading = jnp.transpose(amps_tno, (1, 0, 2)).reshape(tno_size, 3 * tno_size)
    connected = lax.dot_general(
        leading, khatri, (((1,), (1,)), ((), ())), preferred_element_type=jnp.float32
    )
    connected = connected.reshape(tno_size, tno_size, tno_size)
    complete = connected + single_amps[0][None, None, :] * exch_tno[0][:, :, None]
    complete = complete + single_amps[1][None, :, None] * exch_tno[1][:, None, :]
    complete = complete + single_amps[2][:, None, None] * exch_tno[2][None, :, :]
    denominator = (
        tno_levels[:, None, None] + tno_levels[None, :, None] + tno_levels[None, None, :] + shift
    )
    cube_mask = kept_cols[:, None, None] * kept_cols[None, :, None] * kept_cols[None, None, :]
    return jnp.sum(cube_mask * connected * complete / denominator)


def owner_ranks(owners):
    matching = owners[:, None] == owners[None, :]
    position = jnp.arange(owners.shape[0], dtype=jnp.int32)
    earlier = position[None, :] < position[:, None]
    return jnp.sum(jnp.logical_and(matching, earlier), axis=1)


def body(
    triplet_pairs,
    tno_width,
    pair_width,
    pair_coeff,
    pair_amps,
    pair_exch,
    tno_coeff,
    int_left,
    int_right,
    singles,
    tno_energy,
    gap,
):
    owner_count = lax.axis_size("pair")
    pair_dev = pair_coeff.shape[0]
    pno_size = pair_coeff.shape[1]
    domain = pair_coeff.shape[2]
    references = triplet_pairs.reshape(-1)
    ref_count = references.shape[0]
    capacity = (2 * ref_count + owner_count - 1) // owner_count
    kept_rows = (jnp.arange(pno_size, dtype=jnp.int32)[None, :] < pair_width[:, None]).astype(
        jnp.bfloat16
    )
    masked = pair_coeff * kept_rows[:, :, None]
    paired = jnp.concatenate([pair_amps, pair_exch], axis=2)
    chip_refs = gathered_copies(references, "rep", 0)
    owners = chip_refs // pair_dev
    slot_rank = owner_ranks(owners)
    requests = (
        jnp.zeros((owner_count * capacity,), jnp.int32)
        .at[owners * capacity + slot_rank]
        .set(chip_refs % pair_dev)
    )
    requests = requests.reshape(owner_count, capacity)
    asked_rows = lax.all_to_all(requests, "pair", split_axis=0, concat_axis=0, tiled=True)
    replica = lax.axis_index("rep")
    coeff_part = lax.dynamic_slice_in_dim(masked, replica * (domain // 2), domain // 2, 2)
    paired_part = lax.dynamic_slice_in_dim(paired, replica * pno_size, pno_size, 2)
    got_coeff, got_paired = in_one_piece(
        (coeff_part[asked_rows], paired_part[asked_rows]), "pair", 0, 0, 3
    )
    got_coeff, got_paired = (
        lax.all_gather(got_coeff, "rep", axis=3, tiled=True),
        lax.all_gather(got_paired, "rep", axis=3, tiled=True),
    )
    positions = owners * capacity + slot_rank
    positions = lax.dynamic_slice_in_dim(positions, replica * ref_count, ref_count)
    flat_coeff = got_coeff.reshape(-1, pno_size, domain)
    flat_paired = got_paired.reshape(-1, pno_size, 2 * pno_size)
    trips = tno_coeff.shape[0]
    coeff_trip = flat_coeff[positions].reshape(trips, 3, pno_size, domain)
    paired_trip = flat_paired[positions].reshape(trips, 3, pno_size, 2 * pno_size)

    def single_triplet(items):
        return projected_energy(*items)

    energies = lax.map(
        single_triplet,
        (
            coeff_trip,
            paired_trip,
            tno_coeff,
            tno_width,
            int_left,
            int_right,
            singles,
            tno_energy,
            gap,
        ),
    )
    shares = jnp.repeat(energies / 3.0, 3)
    all_pairs = jnp.arange(owner_count * pair_dev, dtype=jnp.int32)
    dense = jnp.sum(
        jnp.where(references[:, None] == all_pairs[None, :], shares[:, None], 0.0), axis=0
    )
    owned = sum_at_owner(dense, "pair", 0)
    pair_energy = gathered_total(owned, "rep")
    return (energies, pair_energy)


def solution(mesh):
    placed = (
        P(("pair", "rep"), None),
        P(("pair", "rep")),
        P("pair"),
        P("pair", None, None),
        P("pair", None, None),
        P("pair", None, None),
        P(("pair", "rep"), None, None),
        P(("pair", "rep"), None, None, None),
        P(("pair", "rep"), None, None, None),
        P(("pair", "rep"), None, None),
        P(("pair", "rep"), None),
        P(("pair", "rep")),
    )
    return jax.shard_map(
        body, mesh=mesh, in_specs=placed, out_specs=(P(("pair", "rep")), P("pair")), check_vma=False
    )
```

profile of v0, /device:TPU:1, one launch (start us, length us, event | category | flops | bytes accessed | tf_op | source)
XLA Modules:
  0.0 379.9 jit_solution(9890772449602783620)
XLA Ops:
  8.2 4.7 %all_to_all.29 = s32[2,1,24]{2,1,0:T(1,128)S(1)} all-to-all(s32[2,1,24]{2,1,0:T(1,128)S(1)} %broadcast_in_dim.33), channel_id=1, replica_groups=mesh['pair'=64,'rep'=2] {'rep'}, dimensions={0} | all-to-all | bytes 384 | tf_op jit(solution)/shard_map/all_to_all | solution.py:15
  15.9 11.2 %all-to-all-start.1 = ((s32[64,1,1]{2,1,0:T(1,128)}), s32[64,1,1]{2,1,0:T(1,128)S(1)}, u32[]{:S(2)}, u32[]{:S(2)}) async-start(s32[64,1,1]{2,1,0:T(1,128)} %copy.64), calls=%async_computation.1 | async-start | bytes 65536 | tf_op jit(solution)/shard_map/all_to_all | solution.py:126
  27.9 4.0 %dynamic-slice_multiply_fusion = bf16[64,64,512]{2,1,0:T(8,128)(2,1)} fusion(bf16[64,64,1024]{2,1,0:T(8,128)(2,1)} %param.17, s32[]{:T(128)S(6)} %select_n.62, bf16[64,64]{1,0:T(8,128)(2,1)S(1)} %fusion.24), kind=kLoop, calls=%fused_computation.44 | loop fusion | flops 8388608 | bytes 8396804 | tf_op jit(solution)/shard_map/mul | solution.py:115
  33.0 2.5 all-to-all-done.1
  37.5 5.0 %gather_fusion = bf16[64,64,512]{2,1,0:T(8,128)(2,1)} fusion(bf16[64,64,512]{2,1,0:T(8,128)(2,1)} %dynamic-slice_multiply_fusion, s32[1024]{0:T(1024)S(1)} %pad_clamp_fusion.1), kind=kCustom, calls=%fused_computation | custom fusion | bytes 8388864 | tf_op jit(solution)/shard_map/gather | solution.py:131
  42.5 3.0 pad_maximum_fusion
  45.5 68.6 %all_to_all.30 = bf16[64,1,64,576]{3,2,1,0:T(8,128)(2,1)S(1)} all-to-all(bf16[64,1,64,576]{3,2,1,0:T(8,128)(2,1)S(1)} %pad_maximum_fusion), channel_id=1, replica_groups=mesh['pair'=64,'rep'=2] {'pair'}, dimensions={0} | all-to-all | bytes 9437184 | tf_op jit(solution)/shard_map/all_to_all | solution.py:25
  119.2 4.6 %split.8 = bf16[64,1,64,512]{3,2,1,0:T(8,128)(2,1)} slice(bf16[64,1,64,576]{3,2,1,0:T(8,128)(2,1)} %copy-done), slice={[0:64], [0:1], [0:64], [0:512]} | slice | bytes 8388608 | tf_op jit(solution)/shard_map/split | solution.py:26
  124.0 7.7 %all-gather.6.cloned.1.call-done = bf16[64,1,64,128]{2,0,1,3:T(8,128)(2,1)} async-done(((bf16[64,1,64,64]{2,0,1,3:T(8,128)(2,1)}), bf16[64,1,64,128]{2,0,1,3:T(8,128)(2,1)}) %all-gather.6.cloned.1.call-update) | async-done | bytes 1048592 | tf_op jit(solution)/shard_map/all_gather | solution.py:135
  131.7 3.3 copy.66
  136.4 20.9 %all-gather.4.cloned.1.call-done = bf16[64,1,64,1024]{3,2,1,0:T(8,128)(2,1)} async-done(((bf16[64,1,64,512]{3,2,1,0:T(8,128)(2,1)}), bf16[64,1,64,1024]{3,2,1,0:T(8,128)(2,1)}) %all-gather.4.cloned.1.call-update) | async-done | bytes 8388624 | tf_op jit(solution)/shard_map/all_gather | solution.py:134
  157.3 4.1 %gather_fusion.2 = bf16[24,64,1024]{2,1,0:T(8,128)(2,1)S(1)} fusion(bf16[64,64,1024]{2,1,0:T(8,128)(2,1)} %bitcast.122, s32[1024]{0:T(1024)S(1)} %pad_clamp_fusion), kind=kCustom, calls=%fused_computation.2 | custom fusion | bytes 6291552 | tf_op jit(solution)/shard_map/gather | solution.py:142
  161.4 186.2 %while.10 = (s32[]{:T(128)}, f32[8]{0:T(128)}, s32[8]{0:T(128)S(1)}, bf16[8,3,64,1024]{3,2,1,0:T(8,128)(2,1)S(1)}, bf16[8,1024,128]{2,1,0:T(8,128)(2,1)}, /*inde...) while((s32[]{:T(128)}, f32[8]{0:T(128)}, ...), condition=%wide.region_4.5_spmd, body=%wide.region_2.4_spmd.sunk | while | flops 1732485504 | bytes 3848877 | solution.py:148
  172.0 11.5 %fusion.53 = f32[]{:T(128)} fusion(f32[]{:T(128)} %bitcast.106, f32[128]{0:T(128)} %copy-done.3, f32[128,128]{0,1:T(8,128)} %broadcast_add_fusion.2, f32[128,128]{1,0:T(8,128)} %copy.80, f32[128]{0:T(128)} %get-tuple-element.239, f32[128,128]{1,0:T(8,128)S(1)} %copy.81, f32[128]{0:T(128)} %get-tuple-element.241, f32[128,128]{0,1:T(8,128)} %get-tuple-element.242, ...), kind=kOutput, calls=%fused_computation.8.clone.1 | convolution fusion | flops 1663041536 | bytes 625160 | tf_op jit(solution)/shard_map/while/body/eval_jaxpr/dot_general | solution.py:70
  195.3 11.5 %fusion.53 = f32[]{:T(128)} fusion(f32[]{:T(128)} %bitcast.106, f32[128]{0:T(128)} %copy-done.3, f32[128,128]{0,1:T(8,128)} %broadcast_add_fusion.2, f32[128,128]{1,0:T(8,128)} %copy.80, f32[128]{0:T(128)} %get-tuple-element.239, f32[128,128]{1,0:T(8,128)S(1)} %copy.81, f32[128]{0:T(128)} %get-tuple-element.241, f32[128,128]{0,1:T(8,128)} %get-tuple-element.242, ...), kind=kOutput, calls=%fused_computation.8.clone.1 | convolution fusion | flops 1663041536 | bytes 625160 | tf_op jit(solution)/shard_map/while/body/eval_jaxpr/dot_general | solution.py:70
  218.5 11.5 %fusion.53 = f32[]{:T(128)} fusion(f32[]{:T(128)} %bitcast.106, f32[128]{0:T(128)} %copy-done.3, f32[128,128]{0,1:T(8,128)} %broadcast_add_fusion.2, f32[128,128]{1,0:T(8,128)} %copy.80, f32[128]{0:T(128)} %get-tuple-element.239, f32[128,128]{1,0:T(8,128)S(1)} %copy.81, f32[128]{0:T(128)} %get-tuple-element.241, f32[128,128]{0,1:T(8,128)} %get-tuple-element.242, ...), kind=kOutput, calls=%fused_computation.8.clone.1 | convolution fusion | flops 1663041536 | bytes 625160 | tf_op jit(solution)/shard_map/while/body/eval_jaxpr/dot_general | solution.py:70
  241.8 11.5 %fusion.53 = f32[]{:T(128)} fusion(f32[]{:T(128)} %bitcast.106, f32[128]{0:T(128)} %copy-done.3, f32[128,128]{0,1:T(8,128)} %broadcast_add_fusion.2, f32[128,128]{1,0:T(8,128)} %copy.80, f32[128]{0:T(128)} %get-tuple-element.239, f32[128,128]{1,0:T(8,128)S(1)} %copy.81, f32[128]{0:T(128)} %get-tuple-element.241, f32[128,128]{0,1:T(8,128)} %get-tuple-element.242, ...), kind=kOutput, calls=%fused_computation.8.clone.1 | convolution fusion | flops 1663041536 | bytes 625160 | tf_op jit(solution)/shard_map/while/body/eval_jaxpr/dot_general | solution.py:70
  265.1 11.5 %fusion.53 = f32[]{:T(128)} fusion(f32[]{:T(128)} %bitcast.106, f32[128]{0:T(128)} %copy-done.3, f32[128,128]{0,1:T(8,128)} %broadcast_add_fusion.2, f32[128,128]{1,0:T(8,128)} %copy.80, f32[128]{0:T(128)} %get-tuple-element.239, f32[128,128]{1,0:T(8,128)S(1)} %copy.81, f32[128]{0:T(128)} %get-tuple-element.241, f32[128,128]{0,1:T(8,128)} %get-tuple-element.242, ...), kind=kOutput, calls=%fused_computation.8.clone.1 | convolution fusion | flops 1663041536 | bytes 625160 | tf_op jit(solution)/shard_map/while/body/eval_jaxpr/dot_general | solution.py:70
  288.4 11.5 %fusion.53 = f32[]{:T(128)} fusion(f32[]{:T(128)} %bitcast.106, f32[128]{0:T(128)} %copy-done.3, f32[128,128]{0,1:T(8,128)} %broadcast_add_fusion.2, f32[128,128]{1,0:T(8,128)} %copy.80, f32[128]{0:T(128)} %get-tuple-element.239, f32[128,128]{1,0:T(8,128)S(1)} %copy.81, f32[128]{0:T(128)} %get-tuple-element.241, f32[128,128]{0,1:T(8,128)} %get-tuple-element.242, ...), kind=kOutput, calls=%fused_computation.8.clone.1 | convolution fusion | flops 1663041536 | bytes 625160 | tf_op jit(solution)/shard_map/while/body/eval_jaxpr/dot_general | solution.py:70
  311.7 11.5 %fusion.53 = f32[]{:T(128)} fusion(f32[]{:T(128)} %bitcast.106, f32[128]{0:T(128)} %copy-done.3, f32[128,128]{0,1:T(8,128)} %broadcast_add_fusion.2, f32[128,128]{1,0:T(8,128)} %copy.80, f32[128]{0:T(128)} %get-tuple-element.239, f32[128,128]{1,0:T(8,128)S(1)} %copy.81, f32[128]{0:T(128)} %get-tuple-element.241, f32[128,128]{0,1:T(8,128)} %get-tuple-element.242, ...), kind=kOutput, calls=%fused_computation.8.clone.1 | convolution fusion | flops 1663041536 | bytes 625160 | tf_op jit(solution)/shard_map/while/body/eval_jaxpr/dot_general | solution.py:70
  334.9 11.5 %fusion.53 = f32[]{:T(128)} fusion(f32[]{:T(128)} %bitcast.106, f32[128]{0:T(128)} %copy-done.3, f32[128,128]{0,1:T(8,128)} %broadcast_add_fusion.2, f32[128,128]{1,0:T(8,128)} %copy.80, f32[128]{0:T(128)} %get-tuple-element.239, f32[128,128]{1,0:T(8,128)S(1)} %copy.81, f32[128]{0:T(128)} %get-tuple-element.241, f32[128,128]{0,1:T(8,128)} %get-tuple-element.242, ...), kind=kOutput, calls=%fused_computation.8.clone.1 | convolution fusion | flops 1663041536 | bytes 625160 | tf_op jit(solution)/shard_map/while/body/eval_jaxpr/dot_general | solution.py:70
  349.9 10.1 %all-to-all-start.3 = ((f32[64,1,64]{2,1,0:T(1,128)}), f32[64,1,64]{2,1,0:T(1,128)S(1)}, u32[]{:S(2)}, u32[]{:S(2)}) async-start(f32[64,1,64]{2,1,0:T(1,128)} %all_to_all.23), calls=%async_computation.3 | async-start | bytes 65536 | tf_op jit(solution)/shard_map/all_to_all | solution.py:37
  361.9 6.5 %all-to-all-done.3 = f32[64,1,64]{2,1,0:T(1,128)S(1)} async-done(((f32[64,1,64]{2,1,0:T(1,128)}), f32[64,1,64]{2,1,0:T(1,128)S(1)}, u32[]{:S(2)}, u32[]{:S(2)}) %all-to-all-start.3) | async-done | bytes 16416 | tf_op jit(solution)/shard_map/all_to_all | solution.py:37
  368.7 3.7 all-reduce
  (291 shorter events, 111.7 us)
Async XLA Ops:
  7.2 24.8 %copy-start.1 = (bf16[64,64,64]{2,1,0:T(8,128)(2,1)S(1)}, bf16[64,64,64]{2,1,0:T(8,128)(2,1)}, u32[]{:S(2)}) copy-start(bf16[64,64,64]{2,1,0:T(8,128)(2,1)} %param.19) | copy-start | bytes 1572868
  7.2 24.8 %copy-start.2 = (bf16[64,64,64]{2,1,0:T(8,128)(2,1)S(1)}, bf16[64,64,64]{2,1,0:T(8,128)(2,1)}, u32[]{:S(2)}) copy-start(bf16[64,64,64]{2,1,0:T(8,128)(2,1)} %param.18) | copy-start | bytes 1572868
  8.2 19.0 %copy-start.5 = (s32[24]{0:T(128)}, s32[24]{0:T(128)S(1)}, u32[]{:S(2)}) copy-start(s32[24]{0:T(128)S(1)} %broadcast_in_dim.32) | copy-start | bytes 292
  15.9 19.6 %all-to-all-start.1 = ((s32[64,1,1]{2,1,0:T(1,128)}), s32[64,1,1]{2,1,0:T(1,128)S(1)}, u32[]{:S(2)}, u32[]{:S(2)}) async-start(s32[64,1,1]{2,1,0:T(1,128)} %copy.64), calls=%async_computation.1 | async-start | bytes 65536 | tf_op jit(solution)/shard_map/all_to_all | solution.py:126
  27.2 104.6 %all-gather.6.cloned.1.call-start = ((), (), s32[]{:S(2)}) async-start(), calls=%async_computation.5 | async-start | bytes 3145728 | tf_op jit(solution)/shard_map/all_gather | solution.py:135
  119.0 38.3 %all-gather.4.cloned.1.call-start = ((), (), s32[]{:S(2)}) async-start(), calls=%async_computation.4 | async-start | bytes 12582912 | tf_op jit(solution)/shard_map/all_gather | solution.py:134
  123.9 37.5 %copy-start.6 = (s32[8]{0:T(128)S(1)}, s32[8]{0:T(128)}, u32[]{:S(2)}) copy-start(s32[8]{0:T(128)} %param.15) | copy-start | bytes 100
  123.9 37.5 %copy-start.8 = (f32[8]{0:T(128)S(1)}, f32[8]{0:T(128)}, u32[]{:S(2)}) copy-start(f32[8]{0:T(128)} %param.25) | copy-start | bytes 100
  172.0 12.8 %copy-start.7 = (s32[8]{0:T(128)S(1)}, s32[8]{0:T(128)}, u32[]{:S(2)}) copy-start(s32[8]{0:T(128)} %get-tuple-element.317) | copy-start | bytes 100 | tf_op jit(solution)/shard_map/while
  172.0 12.7 %copy-start.9 = (f32[8]{0:T(128)S(1)}, f32[8]{0:T(128)}, u32[]{:S(2)}) copy-start(f32[8]{0:T(128)} %get-tuple-element.334) | copy-start | bytes 100 | tf_op jit(solution)/shard_map/while
  195.2 12.8 %copy-start.7 = (s32[8]{0:T(128)S(1)}, s32[8]{0:T(128)}, u32[]{:S(2)}) copy-start(s32[8]{0:T(128)} %get-tuple-element.317) | copy-start | bytes 100 | tf_op jit(solution)/shard_map/while
  195.3 12.7 %copy-start.9 = (f32[8]{0:T(128)S(1)}, f32[8]{0:T(128)}, u32[]{:S(2)}) copy-start(f32[8]{0:T(128)} %get-tuple-element.334) | copy-start | bytes 100 | tf_op jit(solution)/shard_map/while
  218.5 12.8 %copy-start.7 = (s32[8]{0:T(128)S(1)}, s32[8]{0:T(128)}, u32[]{:S(2)}) copy-start(s32[8]{0:T(128)} %get-tuple-element.317) | copy-start | bytes 100 | tf_op jit(solution)/shard_map/while
  218.5 12.7 %copy-start.9 = (f32[8]{0:T(128)S(1)}, f32[8]{0:T(128)}, u32[]{:S(2)}) copy-start(f32[8]{0:T(128)} %get-tuple-element.334) | copy-start | bytes 100 | tf_op jit(solution)/shard_map/while
  241.8 12.8 %copy-start.7 = (s32[8]{0:T(128)S(1)}, s32[8]{0:T(128)}, u32[]{:S(2)}) copy-start(s32[8]{0:T(128)} %get-tuple-element.317) | copy-start | bytes 100 | tf_op jit(solution)/shard_map/while
  241.8 12.7 %copy-start.9 = (f32[8]{0:T(128)S(1)}, f32[8]{0:T(128)}, u32[]{:S(2)}) copy-start(f32[8]{0:T(128)} %get-tuple-element.334) | copy-start | bytes 100 | tf_op jit(solution)/shard_map/while
  265.1 12.8 %copy-start.7 = (s32[8]{0:T(128)S(1)}, s32[8]{0:T(128)}, u32[]{:S(2)}) copy-start(s32[8]{0:T(128)} %get-tuple-element.317) | copy-start | bytes 100 | tf_op jit(solution)/shard_map/while
  265.1 12.7 %copy-start.9 = (f32[8]{0:T(128)S(1)}, f32[8]{0:T(128)}, u32[]{:S(2)}) copy-start(f32[8]{0:T(128)} %get-tuple-element.334) | copy-start | bytes 100 | tf_op jit(solution)/shard_map/while
  288.4 12.8 %copy-start.7 = (s32[8]{0:T(128)S(1)}, s32[8]{0:T(128)}, u32[]{:S(2)}) copy-start(s32[8]{0:T(128)} %get-tuple-element.317) | copy-start | bytes 100 | tf_op jit(solution)/shard_map/while
  288.4 12.7 %copy-start.9 = (f32[8]{0:T(128)S(1)}, f32[8]{0:T(128)}, u32[]{:S(2)}) copy-start(f32[8]{0:T(128)} %get-tuple-element.334) | copy-start | bytes 100 | tf_op jit(solution)/shard_map/while
  311.6 12.8 %copy-start.7 = (s32[8]{0:T(128)S(1)}, s32[8]{0:T(128)}, u32[]{:S(2)}) copy-start(s32[8]{0:T(128)} %get-tuple-element.317) | copy-start | bytes 100 | tf_op jit(solution)/shard_map/while
  311.6 12.7 %copy-start.9 = (f32[8]{0:T(128)S(1)}, f32[8]{0:T(128)}, u32[]{:S(2)}) copy-start(f32[8]{0:T(128)} %get-tuple-element.334) | copy-start | bytes 100 | tf_op jit(solution)/shard_map/while
  334.9 12.8 %copy-start.7 = (s32[8]{0:T(128)S(1)}, s32[8]{0:T(128)}, u32[]{:S(2)}) copy-start(s32[8]{0:T(128)} %get-tuple-element.317) | copy-start | bytes 100 | tf_op jit(solution)/shard_map/while
  349.9 18.6 %all-to-all-start.3 = ((f32[64,1,64]{2,1,0:T(1,128)}), f32[64,1,64]{2,1,0:T(1,128)S(1)}, u32[]{:S(2)}, u32[]{:S(2)}) async-start(f32[64,1,64]{2,1,0:T(1,128)} %all_to_all.23), calls=%async_computation.3 | async-start | bytes 65536 | tf_op jit(solution)/shard_map/all_to_all | solution.py:37
  (34 other events, 148.2 us)
Sparse Core Ops, SparseCore 0:
  119.1 12.5 all-gather.5
  133.4 23.8 all-gather.3
where the time goes:
time: 382 us; the launch traced here: 380 us
  matrix products  112 us (29%)
  local copies, waits for them, and re-layouts  91.4 us (24%)
  blocking collectives  77.1 us (20%)
  waiting for transfers between devices  37.6 us (10%)
  other arithmetic  24.2 us (6%)
  starting transfers between devices  21.6 us (6%)
  between operations  14.9 us (4%)
    dot_general x8, matrix products, projected_energy(): lax.dot_general(leading, khatri, (((1,), (1,)), ((), ())), preferred_elem...  92.3 us
    all_to_all x1, blocking collectives, in_one_piece(): lax.all_to_all(both, axis, split_axis=split_dim, concat_axis=concat_dim,...  68.6 us
    all_gather x1, waiting for transfers between devices, body(): lax.all_gather(got_coeff, 'rep', axis=3, tiled=True)  20.9 us
    dynamic_slice x24, local copies, waits for them, and re-layouts, body(): lax.map(single_triplet, (coeff_trip, paired_trip, tno_coeff, tno_width, i...  17.4 us
    mul x16, local copies, waits for them, and re-layouts, projected_energy(): single_amps[0][None, None, :] * exch_tno[0][:, :, None]  15.7 us
    all_to_all x1, starting transfers between devices, body(): lax.all_to_all(requests, 'pair', split_axis=0, concat_axis=0, tiled=True)  11.2 us
    all_to_all x1, starting transfers between devices, sum_at_owner(): parts = lax.all_to_all(cut_along(x, dim, size), axis, 0, 0, tiled=True)  10.1 us
    dot_general x8, matrix products, projected_energy(): jnp.einsum('xad,db->xab', pno_coeff, tno_kept, preferred_element_type=jnp...  9.63 us
  transfers between devices with their start and end apart: 4, of which 4 were waited for; matrix products, arithmetic and copies ran while one was open for 4% of the time, Pallas kernels for 0%

commit v1 on v0

v1 whole, which is shorter than its diff:
```python
import jax
import jax.numpy as jnp
from jax import lax
from jax.experimental import pallas as pl
from jax.experimental.pallas import tpu as pltpu
from jax.sharding import PartitionSpec as P

BOTH = ("pair", "rep")


def slots_kernel(rows, coeff, blocks, out, buf, got, put, *, halves):
    slots, slot_rows, lanes = buf.shape
    pno = coeff.shape[1]
    dom_part = coeff.shape[2] // halves
    pieces = dom_part // lanes
    pair_rows = pno // halves
    rep = rows[slots]

    def start(s, _):
        row = rows[s]
        for piece in range(pieces):
            pltpu.make_async_copy(
                coeff.at[row, :, pl.ds(rep * dom_part + piece * lanes, lanes)],
                buf.at[s, pl.ds(piece * pno, pno), :],
                got.at[s],
            ).start()
        pltpu.make_async_copy(
            blocks.at[row, pl.ds(rep * pair_rows, pair_rows), :],
            buf.at[s, pl.ds(pieces * pno, pair_rows), :],
            got.at[s],
        ).start()
        return 0

    def forward(s, _):
        pltpu.make_async_copy(out.at[s], buf.at[s], got.at[s]).wait()
        pltpu.make_async_copy(buf.at[s], out.at[s], put.at[s]).start()
        return 0

    def finish(s, _):
        pltpu.make_async_copy(buf.at[s], out.at[s], put.at[s]).wait()
        return 0

    lax.fori_loop(0, slots, start, 0)
    lax.fori_loop(0, slots, forward, 0)
    lax.fori_loop(0, slots, finish, 0)


def send_slots(rows, coeff, blocks, halves):
    slots = rows.shape[0] - 1
    _, pno, domain = coeff.shape
    lanes = blocks.shape[2]
    slot_rows = pno * (domain // halves // lanes) + pno // halves
    shape = (slots, slot_rows, lanes)
    return pl.pallas_call(
        lambda *refs: slots_kernel(*refs, halves=halves),
        grid_spec=pltpu.PrefetchScalarGridSpec(
            num_scalar_prefetch=1,
            grid=(),
            in_specs=[pl.BlockSpec(memory_space=pl.ANY), pl.BlockSpec(memory_space=pl.ANY)],
            out_specs=pl.BlockSpec(memory_space=pl.ANY),
            scratch_shapes=[
                pltpu.VMEM(shape, jnp.bfloat16),
                pltpu.SemaphoreType.DMA((slots,)),
                pltpu.SemaphoreType.DMA((slots,)),
            ],
        ),
        out_shape=jax.ShapeDtypeStruct(shape, jnp.bfloat16),
        name="slots",
    )(rows, coeff, blocks)


def dot_nt(x, y):
    return lax.dot_general(x, y, (((1,), (1,)), ((), ())), preferred_element_type=jnp.float32)


def dot_tn(x, y):
    return lax.dot_general(x, y, (((0,), (0,)), ((), ())), preferred_element_type=jnp.float32)


def dot_tt(x, y):
    return lax.dot_general(x, y, (((0,), (1,)), ((), ())), preferred_element_type=jnp.float32)


def down_rows(row):
    size = row.shape[1]
    return jnp.transpose(jnp.broadcast_to(row, (size, size)))


STEP = 8


def energy_kernel(
    meta, levels_s, singles_s, gap_s,
    own0, own1, own2, far0, far1, far2, tno, left, right, singles, levels,
    out,
    left_t, right_t, weights, exch0, exch1, exch2, single0, base, ix,
):
    t = pl.program_id(0)
    trips = levels_s.shape[0]
    width = meta[4 * trips - trips + t]
    rep = meta[4 * trips]
    own = (own0, own1, own2)
    far = (far0, far1, far2)
    size = tno.shape[2]
    half_dom = tno.shape[1] // 2
    lanes = own0.shape[2]
    pieces = half_dom // lanes
    pno = (own0.shape[1] * 2) // (2 * pieces + 1)
    part = pno // 2

    def stacked(refs):
        rows = []
        for ref in refs:
            cols = [ref[0, k * pno : (k + 1) * pno, :] for k in range(pieces)]
            rows.append(jnp.concatenate(cols, axis=1))
        return jnp.concatenate(rows, axis=0)

    inter = jnp.dot(
        stacked(own), tno[0, pl.ds(rep * half_dom, half_dom), :], preferred_element_type=jnp.float32
    )
    inter += jnp.dot(
        stacked(far),
        tno[0, pl.ds((1 - rep) * half_dom, half_dom), :],
        preferred_element_type=jnp.float32,
    )
    lane = lax.broadcasted_iota(jnp.int32, inter.shape, 1)
    inter = jnp.where(lane < width, inter, 0.0).astype(jnp.bfloat16)
    row_ok = lax.broadcasted_iota(jnp.int32, (size, size), 0) < width
    eye = (
        lax.broadcasted_iota(jnp.int32, (size, size), 0)
        == lax.broadcasted_iota(jnp.int32, (size, size), 1)
    ).astype(jnp.float32).astype(jnp.bfloat16)
    weights[...] = jnp.zeros(weights.shape, weights.dtype)
    exch = (exch0, exch1, exch2)
    spots = ((0, 256), (128, 384), (512, 640))
    for x in range(3):
        ix[pl.ds(rep * part, part), :] = own[x][0, pieces * pno : pieces * pno + part, :]
        ix[pl.ds((1 - rep) * part, part), :] = far[x][0, pieces * pno : pieces * pno + part, :]
        inter_x = inter[x * pno : (x + 1) * pno, :]
        halfway = dot_tn(inter_x, ix[...]).astype(jnp.bfloat16)
        amps = dot_tt(inter_x, halfway[:, :pno]).astype(jnp.bfloat16)
        exch[x][...] = dot_tt(inter_x, halfway[:, pno:])
        weights[spots[x][0] : spots[x][0] + size, :size] = amps
        weights[spots[x][1] : spots[x][1] + size, size:] = amps
        left_t[:, x * size : (x + 1) * size] = jnp.where(row_ok, dot_nt(eye, left[0, x]), 0.0)
        right_t[:, x * size : (x + 1) * size] = jnp.where(
            row_ok, dot_nt(eye, right[0, x]), 0.0
        ).astype(jnp.bfloat16)
    single0[...] = down_rows(singles[0, 0:1, :])
    base[...] = down_rows(levels[0, 0:1, :]) + levels[0, 0:1, :] + gap_s[t]
    single2 = singles[0, 2:3, :]

    def block(i, total):
        b0 = i * STEP
        left_rows = left_t[pl.ds(b0, STEP), :]
        exch0_rows = exch0[pl.ds(b0, STEP), :]
        exch2_cols = pltpu.roll(exch2[...], size - b0, 1)
        right_all = right_t[...]
        for j in range(0, STEP, 2):
            first = right_all * jnp.broadcast_to(left_rows[j : j + 1, :], right_all.shape).astype(
                jnp.bfloat16
            )
            second = right_all * jnp.broadcast_to(
                left_rows[j + 1 : j + 2, :], right_all.shape
            ).astype(jnp.bfloat16)
            khatri = jnp.concatenate(
                [first[:, :256], second[:, :256], first[:, 256:], second[:, 256:]], axis=1
            )
            both = jnp.dot(khatri, weights[...], preferred_element_type=jnp.float32)
            for h in range(2):
                b = b0 + j + h
                connected = both[:, h * size : (h + 1) * size]
                complete = connected + singles_s[t, 1, b] * exch1[...]
                complete += single0[...] * exch0_rows[j + h : j + h + 1, :]
                complete += exch2_cols[:, j + h : j + h + 1] * single2
                term = connected * complete / (base[...] + levels_s[t, b])
                total += jnp.sum(term.reshape(size // 8, 8, size), axis=0)
        return total

    blocks = (width + STEP - 1) // STEP
    out[0] = lax.fori_loop(0, blocks, block, jnp.zeros((8, size), jnp.float32))


def triplet_energies(meta, own, far, tno, left, right, singles, levels, gap):
    trips, _, size = tno.shape
    slot = own.shape[1:]

    def pair_spec(x):
        return pl.BlockSpec((1, *slot), lambda t, meta, *_: (meta[3 * t + x], 0, 0))

    def trip_spec(shape):
        return pl.BlockSpec((1, *shape), lambda t, *_: (t,) + (0,) * len(shape))

    return pl.pallas_call(
        energy_kernel,
        grid_spec=pltpu.PrefetchScalarGridSpec(
            num_scalar_prefetch=4,
            grid=(trips,),
            in_specs=[pair_spec(x) for x in range(3)]
            + [pair_spec(x) for x in range(3)]
            + [
                trip_spec(tno.shape[1:]),
                trip_spec(left.shape[1:]),
                trip_spec(right.shape[1:]),
                trip_spec(singles.shape[1:]),
                trip_spec((1, size)),
            ],
            out_specs=trip_spec((8, size)),
            scratch_shapes=[
                pltpu.VMEM((size, 3 * size), jnp.float32),
                pltpu.VMEM((size, 3 * size), jnp.bfloat16),
                pltpu.VMEM((6 * size, 2 * size), jnp.bfloat16),
                pltpu.VMEM((size, size), jnp.float32),
                pltpu.VMEM((size, size), jnp.float32),
                pltpu.VMEM((size, size), jnp.float32),
                pltpu.VMEM((size, size), jnp.float32),
                pltpu.VMEM((size, size), jnp.float32),
                pltpu.VMEM((size // 2, size), jnp.bfloat16),
            ],
        ),
        out_shape=jax.ShapeDtypeStruct((trips, 8, size), jnp.float32),
        compiler_params=pltpu.CompilerParams(dimension_semantics=("arbitrary",)),
        name="energy",
    )(
        meta, levels, singles, gap,
        own, own, own, far, far, far, tno, left, right, singles, levels.reshape(trips, 1, size),
    )


def body(
    triplet_pairs, tno_width, pair_width, pair_coeff, pair_amps, pair_exch, tno_coeff,
    int_left, int_right, singles, tno_energy, gap,
):
    owners_n = lax.axis_size("pair")
    reps = lax.axis_size("rep")
    pair_dev, pno, _ = pair_coeff.shape
    rep = lax.axis_index("rep")
    references = triplet_pairs.reshape(-1)
    owners = references // pair_dev
    at_owner = owners[None, :] == jnp.arange(owners_n, dtype=jnp.int32)[:, None]

    wanted = jnp.sum(jnp.where(at_owner, references % pair_dev + 1, 0), axis=1)
    wanted = jnp.broadcast_to(wanted[:, None], (owners_n, reps)).reshape(-1, 1)
    asked = lax.all_to_all(wanted, BOTH, 0, 0, tiled=True)
    asked = jnp.max(asked.reshape(owners_n, reps), axis=1) - 1

    kept = jnp.arange(pno, dtype=jnp.int32)[None, :] < pair_width[:, None]
    kept = kept[:, :, None] & kept[:, None, :]
    zero = jnp.zeros((), pair_amps.dtype)
    blocks = jnp.concatenate(
        [jnp.where(kept, pair_amps, zero), jnp.where(kept, pair_exch, zero)], axis=2
    )
    rows = jnp.concatenate([jnp.maximum(asked, 0), rep[None].astype(jnp.int32)])
    sent = send_slots(rows, pair_coeff, blocks, reps)
    got = lax.all_to_all(sent, "pair", 0, 0, tiled=True)
    far = lax.ppermute(got, "rep", [(0, 1), (1, 0)])

    meta = jnp.concatenate([owners, tno_width, rep[None].astype(jnp.int32)])
    partial = triplet_energies(
        meta, got, far, tno_coeff, int_left, int_right, singles, tno_energy, gap
    )
    energies = jnp.sum(partial, axis=(1, 2))

    shares = jnp.repeat(energies / 3.0, 3)
    shares = jnp.sum(jnp.where(at_owner, shares[None, :], 0.0), axis=1)
    shares = jnp.broadcast_to(shares[:, None], (owners_n, reps)).reshape(-1, 1)
    shares = lax.all_to_all(shares, BOTH, 0, 0, tiled=True)
    shares = jnp.sum(shares.reshape(owners_n, reps), axis=1)
    here = asked[None, :] == jnp.arange(pair_dev, dtype=jnp.int32)[:, None]
    pair_energy = jnp.sum(jnp.where(here, shares[None, :], 0.0), axis=1)
    return (energies, pair_energy)


def solution(mesh):
    both = P(BOTH)
    pair = P("pair")
    placed = (both, both, pair, pair, pair, pair, both, both, both, both, both, both)
    return jax.shard_map(
        body, mesh=mesh, in_specs=placed, out_specs=(both, pair), check_vma=False
    )
```

time: 382 us -> 192 us (0.50)
  matrix products: 112 us -> 0 us
  local copies, waits for them, and re-layouts: 91.4 us -> 7.17 us
  Pallas kernels: 0 us -> 72.9 us
  waiting for transfers between devices: 37.6 us -> 10.5 us
  between operations: 14.9 us -> 0.73 us
  other arithmetic: 24.2 us -> 11.8 us
  starting transfers between devices: 21.6 us -> 14 us
    dot_general x32 -> x0, matrix products: 112 us -> none  [the longest x8 92.3 us: projected_energy(): lax.dot_general(leading, khatri, (((1,), (1,)), ((), ())), preferred_elem...]
    pallas_call x0 -> x2, Pallas kernels: none -> 72.9 us  [the longest x1 65.3 us: triplet_energies(): pl.pallas_call(energy_kernel, grid_spec=pltpu.PrefetchScalarGridSpec(num_...]
    mul x48 -> x0, local copies, waits for them, and re-layouts: 29 us -> none  [the longest x16 15.7 us: projected_energy(): single_amps[0][None, None, :] * exch_tno[0][:, :, None]]
    all_gather x2 -> x0, waiting for transfers between devices: 28.6 us -> none  [the longest x1 20.9 us: body(): lax.all_gather(got_coeff, 'rep', axis=3, tiled=True)]
    dynamic_slice x24 -> x0, local copies, waits for them, and re-layouts: 17.4 us -> none  [body(): lax.map(single_triplet, (coeff_trip, paired_trip, tno_coeff, tno_width, i...]
    gather x4 -> x0, local copies, waits for them, and re-layouts: 11.2 us -> none  [the longest x1 4.98 us: body(): coeff_part[asked_rows]]
    all_to_all x2 -> x1, starting transfers between devices: 21.4 us -> 11.5 us  [body(): asked = lax.all_to_all(wanted, BOTH, 0, 0, tiled=True)]
    split x3 -> x0, local copies, waits for them, and re-layouts: 7.19 us -> none  [in_one_piece(): jnp.split(out, [sum(widths[:k]) for k in range(1, len(widths))], axis=along)]
  transfers between devices with their start and end apart: 4 -> 2, of which waited for: 4 -> 2; matrix products, arithmetic and copies ran while one was open for 4% -> 3% of each run, Pallas kernels for 0% -> 0%
where the time goes in v1:
time: 192 us; the launch traced here: 191 us
  blocking collectives  74.3 us (39%)
  Pallas kernels  72.9 us (38%)
  starting transfers between devices  14 us (7%)
  other arithmetic  11.8 us (6%)
  waiting for transfers between devices  10.5 us (5%)
  local copies, waits for them, and re-layouts  7.17 us (4%)
    pallas_call x1, Pallas kernels, triplet_energies(): pl.pallas_call(energy_kernel, grid_spec=pltpu.PrefetchScalarGridSpec(num_...  65.3 us
    all_to_all x1, blocking collectives, body(): got = lax.all_to_all(sent, 'pair', 0, 0, tiled=True)  62.5 us
    all_to_all x1, blocking collectives, body(): shares = lax.all_to_all(shares, BOTH, 0, 0, tiled=True)  11.8 us
    all_to_all x1, starting transfers between devices, body(): asked = lax.all_to_all(wanted, BOTH, 0, 0, tiled=True)  11.5 us
    pallas_call x1, Pallas kernels, send_slots(): pl.pallas_call(lambda *refs: slots_kernel(*refs, halves=halves), grid_spe...  7.53 us
    ppermute x1, waiting for transfers between devices, body(): far = lax.ppermute(got, 'rep', [(0, 1), (1, 0)])  6.34 us
    unnamed x12, local copies, waits for them, and re-layouts  5.67 us
    all_to_all x1, waiting for transfers between devices, body(): asked = lax.all_to_all(wanted, BOTH, 0, 0, tiled=True)  4.12 us
  transfers between devices with their start and end apart: 2, of which 2 were waited for; matrix products, arithmetic and copies ran while one was open for 3% of the time, Pallas kernels for 0%

profile of v1, /device:TPU:1, one launch (start us, length us, event | category | flops | bytes accessed | tf_op | source)
XLA Modules:
  0.0 191.4 jit_solution(16111906590243532909)
XLA Ops:
  0.6 0.8 copy.25
  1.6 0.7 all_to_all.20
  2.4 11.5 %all-to-all-start = ((s32[128,1,1]{2,1,0:T(1,128)}), s32[128,1,1]{2,1,0:T(1,128)S(1)}, u32[]{:S(2)}, u32[]{:S(2)}) async-start(s32[128,1,1]{2,1,0:T(1,128)} %all_to_all.20), calls=%async_computation | async-start | bytes 131072 | tf_op jit(solution)/shard_map/all_to_all | solution.py:244
  13.9 0.7 iota_compare_fusion.1
  14.6 2.9 %and_select_fusion.1 = (bf16[64,64,64]{2,1,0:T(8,128)(2,1)S(1)}, bf16[64,64,64]{2,1,0:T(8,128)(2,1)S(1)}) fusion(bf16[64,64,64]{2,1,0:T(8,128)(2,1)} %param.16, pred[64,64]{1,0:T(8,128)(4,1)S(1)} %iota_compare_fusion.1, bf16[64,64,64]{2,1,0:T(8,128)(2,1)} %param.17), kind=kLoop, calls=%fused_computation.1 | loop fusion | flops 786432 | bytes 2101248 | tf_op jit(solution)/shard_map/jit(_where)/select_n | solution.py:251
  17.5 1.6 pad_maximum_fusion.refs_2_
  19.1 4.1 %all-to-all-done = s32[128,1,1]{2,1,0:T(1,128)S(1)} async-done(((s32[128,1,1]{2,1,0:T(1,128)}), s32[128,1,1]{2,1,0:T(1,128)S(1)}, u32[]{:S(2)}, u32[]{:S(2)}) %all-to-all-start) | async-done | bytes 544 | tf_op jit(solution)/shard_map/all_to_all | solution.py:244
  23.3 2.3 %reduce = s32[128]{0:T(128)S(1)} reduce(s32[128,1,1]{2,1,0:T(1,128)S(1)} %all-to-all-done, s32[]{:T(128)} %constant.36.clone.1), dimensions={1,2}, to_apply=%all_to_all.16.reduce_sub_computation | reduce | bytes 1028 | tf_op jit(solution)/shard_map/all_to_all | solution.py:244
  25.6 0.1 reshape.98
  25.9 0.6 pad_add_fusion.1.refs_0_
  26.5 7.5 %slots.1 = bf16[64,288,128]{2,1,0:T(8,128)(2,1)} custom-call(s32[65]{0:T(128)} %pad_add_fusion.1.refs_0_, bf16[64,64,1024]{2,1,0:T(8,128)(2,1)} %refs_1_.1, bf16[64,64,128]{2,1,0:T(8,128)(2,1)} %pad_maximum_fusion.refs_2_), custom_call_target="tpu_custom_call" | custom-call | tf_op jit(solution)/shard_map/slots/pallas_call | solution.py:54
  34.0 62.5 %all_to_all.25.own0.own1.own2 = bf16[64,288,128]{2,1,0:T(8,128)(2,1)S(1)} all-to-all(bf16[64,288,128]{2,1,0:T(8,128)(2,1)} %slots.1), channel_id=1, replica_groups=mesh['pair'=64,'rep'=2] {'pair'}, dimensions={0} | all-to-all | bytes 9437184 | tf_op jit(solution)/shard_map/all_to_all | solution.py:255
  96.6 2.1 %copy-done = bf16[64,288,128]{2,1,0:T(8,128)(2,1)} copy-done((bf16[64,288,128]{2,1,0:T(8,128)(2,1)}, bf16[64,288,128]{2,1,0:T(8,128)(2,1)S(1)}, u32[]{:S(2)}) %copy-start) | copy-done | bytes 4718616
  98.7 2.5 %collective-permute-start = (bf16[64,288,128]{2,1,0:T(8,128)(2,1)S(1)}, bf16[64,288,128]{2,1,0:T(8,128)(2,1)S(1)}, u32[]{:S(2)}, u32[]{:S(2)}) collective-permute-start(bf16[64,288,128]{2,1,0:T(8,128)(2,1)S(1)} %all_to_all.25.own0.own1.own2), channel_id=1, source_target_pairs={{0,1},{1,0},{2,3},{3,2},{4,5},{5,4},{6,7},{7,6},{8,9},{9,8},{10,11... | collective-permute-start | bytes 14155784 | tf_op jit(solution)/shard_map/ppermute | solution.py:256
  101.2 0.6 copy.27.singles_s.singles
  101.8 0.6 pad_add_fusion.meta
  102.4 6.3 %collective-permute-done.far0.far1.far2 = bf16[64,288,128]{2,1,0:T(8,128)(2,1)S(1)} collective-permute-done((bf16[64,288,128]{2,1,0:T(8,128)(2,1)S(1)}, bf16[64,288,128]{2,1,0:T(8,128)(2,1)S(1)}, u32[]{:S(2)}, u32[]{:S(2)}) %collective-permute-start) | collective-permute-done | bytes 4718624 | tf_op jit(solution)/shard_map/ppermute | solution.py:256
  108.8 2.2 %copy-done.1 = bf16[64,288,128]{2,1,0:T(8,128)(2,1)} copy-done((bf16[64,288,128]{2,1,0:T(8,128)(2,1)}, bf16[64,288,128]{2,1,0:T(8,128)(2,1)S(1)}, u32[]{:S(2)}) %copy-start.1) | copy-done | bytes 4718616
  110.9 65.3 %energy.1 = f32[8,8,128]{2,1,0:T(8,128)} custom-call(s32[33]{0:T(128)} %pad_add_fusion.meta, f32[8,128]{1,0:T(8,128)} %levels_s.1, f32[8,3,128]{2,1,0:T(4,128)} %copy.27.singles_s.singles, f32[8]{0:T(128)} %gap_s.1, bf16[64,288,128]{2,1,0:T(8,128)(2,1)} %copy-done, bf16[64,288,128]{2,1,0:T(8,128)(2,1)} %copy-done, bf16[64,288,128]{2,1,0:T(8,128)(2,1)} %copy-done, ...), custom_call_target="tpu_custom_call" | custom-call | tf_op jit(solution)/shard_map/energy/pallas_call | solution.py:194
  176.3 0.9 reduce_sum.46
  177.6 11.8 %all_to_all.26 = f32[128,1,1]{2,1,0:T(1,128)S(1)} all-to-all(f32[128,1,1]{2,1,0:T(1,128)S(1)} %all_to_all.21), channel_id=1, replica_groups=mesh['pair'=64,'rep'=2] {'pair','rep'}, dimensions={0} | all-to-all | bytes 1024 | tf_op jit(solution)/shard_map/all_to_all | solution.py:267
  189.4 1.0 reduce.1
  190.5 0.1 reshape.100
  190.7 0.6 select_reduce_fusion
  (21 shorter events, 1.0 us)
Async XLA Ops:
  2.4 20.9 %all-to-all-start = ((s32[128,1,1]{2,1,0:T(1,128)}), s32[128,1,1]{2,1,0:T(1,128)S(1)}, u32[]{:S(2)}, u32[]{:S(2)}) async-start(s32[128,1,1]{2,1,0:T(1,128)} %all_to_all.20), calls=%async_computation | async-start | bytes 131072 | tf_op jit(solution)/shard_map/all_to_all | solution.py:244
  34.0 67.2 %copy-start.2 = (f32[8,3,128]{2,0,1:T(8,128)S(1)}, f32[8,3,128]{2,0,1:T(8,128)}, u32[]{:S(2)}) copy-start(f32[8,3,128]{2,0,1:T(8,128)} %param.21) | copy-start | bytes 36868
  34.0 67.8 %copy-start.4 = (s32[8]{0:T(128)S(1)}, s32[8]{0:T(128)}, u32[]{:S(2)}) copy-start(s32[8]{0:T(128)} %param.13) | copy-start | bytes 100
  96.6 2.1 %copy-start = (bf16[64,288,128]{2,1,0:T(8,128)(2,1)}, bf16[64,288,128]{2,1,0:T(8,128)(2,1)S(1)}, u32[]{:S(2)}) copy-start(bf16[64,288,128]{2,1,0:T(8,128)(2,1)S(1)} %all_to_all.25.own0.own1.own2) | copy-start | bytes 14155780
  98.7 10.0 %collective-permute-start = (bf16[64,288,128]{2,1,0:T(8,128)(2,1)S(1)}, bf16[64,288,128]{2,1,0:T(8,128)(2,1)S(1)}, u32[]{:S(2)}, u32[]{:S(2)}) collective-permute-start(bf16[64,288,128]{2,1,0:T(8,128)(2,1)S(1)} %all_to_all.25.own0.own1.own2), channel_id=1, source_target_pairs={{0,1},{1,0},{2,3},{3,2},{4,5},{5,4},{6,7},{7,6},{8,9},{9,8},{10,11... | collective-permute-start | bytes 14155784 | tf_op jit(solution)/shard_map/ppermute | solution.py:256
  108.8 2.2 %copy-start.1 = (bf16[64,288,128]{2,1,0:T(8,128)(2,1)}, bf16[64,288,128]{2,1,0:T(8,128)(2,1)S(1)}, u32[]{:S(2)}) copy-start(bf16[64,288,128]{2,1,0:T(8,128)(2,1)S(1)} %collective-permute-done.far0.far1.far2) | copy-start | bytes 14155780
  177.2 14.2 %copy-start.3 = (f32[8]{0:T(128)}, f32[8]{0:T(128)S(1)}, u32[]{:S(2)}) copy-start(f32[8]{0:T(128)S(1)} %reduce_sum.46) | copy-start | bytes 100

commit v2 on v1

--- a/solution.py
+++ b/solution.py
@@ -87,17 +87,68 @@
 
 
 STEP = 8
+GROUP = 2
+
+
+def prepare_kernel(widths, gap_s, left, right, singles, levels, left_t, right_t, columns):
+    t = pl.program_id(0)
+    size = left.shape[2]
+    rows = lax.broadcasted_iota(jnp.int32, (size, size), 0)
+    row_ok = rows < widths[t]
+    eye = (rows == lax.broadcasted_iota(jnp.int32, (size, size), 1)).astype(jnp.float32)
+    eye = eye.astype(jnp.bfloat16)
+    for x in range(3):
+        left_t[0, x] = jnp.where(row_ok, dot_nt(eye, left[0, x]), 0.0)
+        right_t[0, x] = jnp.where(row_ok, dot_nt(eye, right[0, x]), 0.0)
+    columns[0, 0] = down_rows(singles[0, 0:1, :])
+    columns[0, 1] = down_rows(levels[0, 0:1, :]) + levels[0, 0:1, :] + gap_s[t]
+
+
+def trip_spec(shape):
+    return pl.BlockSpec((1, *shape), lambda t, *_: (t,) + (0,) * len(shape))
+
+
+def prepare(widths, gap, left, right, singles, levels):
+    trips, _, size, _ = left.shape
+    return pl.pallas_call(
+        prepare_kernel,
+        grid_spec=pltpu.PrefetchScalarGridSpec(
+            num_scalar_prefetch=2,
+            grid=(trips,),
+            in_specs=[
+                trip_spec(left.shape[1:]),
+                trip_spec(right.shape[1:]),
+                trip_spec(singles.shape[1:]),
+                trip_spec((1, size)),
+            ],
+            out_specs=[
+                trip_spec((3, size, size)),
+                trip_spec((3, size, size)),
+                trip_spec((2, size, size)),
+            ],
+        ),
+        out_shape=[
+            jax.ShapeDtypeStruct((trips, 3, size, size), jnp.float32),
+            jax.ShapeDtypeStruct((trips, 3, size, size), jnp.float32),
+            jax.ShapeDtypeStruct((trips, 2, size, size), jnp.float32),
+        ],
+        compiler_params=pltpu.CompilerParams(dimension_semantics=("arbitrary",)),
+        cost_estimate=pl.CostEstimate(
+            flops=12 * trips * size**3, bytes_accessed=8 * trips * size**2 * 4, transcendentals=0
+        ),
+        name="prepare",
+    )(widths, gap, left, right, singles, levels.reshape(trips, 1, size))
 
 
 def energy_kernel(
-    meta, levels_s, singles_s, gap_s,
-    own0, own1, own2, far0, far1, far2, tno, left, right, singles, levels,
+    meta, levels_s, singles_s,
+    own0, own1, own2, far0, far1, far2, tno, left_t, right_t, columns, singles,
     out,
-    left_t, right_t, weights, exch0, exch1, exch2, single0, base, ix,
+    weights, exch0, exch1, exch2, connected_s, ix,
 ):
     t = pl.program_id(0)
     trips = levels_s.shape[0]
-    width = meta[4 * trips - trips + t]
+    width = meta[3 * trips + t]
     rep = meta[4 * trips]
     own = (own0, own1, own2)
     far = (far0, far1, far2)
@@ -107,6 +158,7 @@
     pieces = half_dom // lanes
     pno = (own0.shape[1] * 2) // (2 * pieces + 1)
     part = pno // 2
+    pairs = STEP // 2
 
     def stacked(refs):
         rows = []
@@ -125,106 +177,123 @@
     )
     lane = lax.broadcasted_iota(jnp.int32, inter.shape, 1)
     inter = jnp.where(lane < width, inter, 0.0).astype(jnp.bfloat16)
-    row_ok = lax.broadcasted_iota(jnp.int32, (size, size), 0) < width
-    eye = (
-        lax.broadcasted_iota(jnp.int32, (size, size), 0)
-        == lax.broadcasted_iota(jnp.int32, (size, size), 1)
-    ).astype(jnp.float32).astype(jnp.bfloat16)
-    weights[...] = jnp.zeros(weights.shape, weights.dtype)
+
+    @pl.when(t == 0)
+    def _():
+        weights[...] = jnp.zeros(weights.shape, weights.dtype)
+
     exch = (exch0, exch1, exch2)
     spots = ((0, 256), (128, 384), (512, 640))
     for x in range(3):
-        ix[pl.ds(rep * part, part), :] = own[x][0, pieces * pno : pieces * pno + part, :]
-        ix[pl.ds((1 - rep) * part, part), :] = far[x][0, pieces * pno : pieces * pno + part, :]
+        ix[x, pl.ds(rep * part, part), :] = own[x][0, pieces * pno : pieces * pno + part, :]
+        ix[x, pl.ds((1 - rep) * part, part), :] = far[x][0, pieces * pno : pieces * pno + part, :]
+    for x in range(3):
         inter_x = inter[x * pno : (x + 1) * pno, :]
-        halfway = dot_tn(inter_x, ix[...]).astype(jnp.bfloat16)
+        halfway = dot_tn(inter_x, ix[x]).astype(jnp.bfloat16)
         amps = dot_tt(inter_x, halfway[:, :pno]).astype(jnp.bfloat16)
         exch[x][...] = dot_tt(inter_x, halfway[:, pno:])
         weights[spots[x][0] : spots[x][0] + size, :size] = amps
         weights[spots[x][1] : spots[x][1] + size, size:] = amps
-        left_t[:, x * size : (x + 1) * size] = jnp.where(row_ok, dot_nt(eye, left[0, x]), 0.0)
-        right_t[:, x * size : (x + 1) * size] = jnp.where(
-            row_ok, dot_nt(eye, right[0, x]), 0.0
-        ).astype(jnp.bfloat16)
-    single0[...] = down_rows(singles[0, 0:1, :])
-    base[...] = down_rows(levels[0, 0:1, :]) + levels[0, 0:1, :] + gap_s[t]
     single2 = singles[0, 2:3, :]
 
-    def block(i, total):
-        b0 = i * STEP
-        left_rows = left_t[pl.ds(b0, STEP), :]
-        exch0_rows = exch0[pl.ds(b0, STEP), :]
-        exch2_cols = pltpu.roll(exch2[...], size - b0, 1)
-        right_all = right_t[...]
-        for j in range(0, STEP, 2):
-            first = right_all * jnp.broadcast_to(left_rows[j : j + 1, :], right_all.shape).astype(
-                jnp.bfloat16
-            )
-            second = right_all * jnp.broadcast_to(
-                left_rows[j + 1 : j + 2, :], right_all.shape
-            ).astype(jnp.bfloat16)
-            khatri = jnp.concatenate(
-                [first[:, :256], second[:, :256], first[:, 256:], second[:, 256:]], axis=1
-            )
-            both = jnp.dot(khatri, weights[...], preferred_element_type=jnp.float32)
-            for h in range(2):
-                b = b0 + j + h
-                connected = both[:, h * size : (h + 1) * size]
-                complete = connected + singles_s[t, 1, b] * exch1[...]
-                complete += single0[...] * exch0_rows[j + h : j + h + 1, :]
-                complete += exch2_cols[:, j + h : j + h + 1] * single2
-                term = connected * complete / (base[...] + levels_s[t, b])
-                total += jnp.sum(term.reshape(size // 8, 8, size), axis=0)
-        return total
-
-    blocks = (width + STEP - 1) // STEP
-    out[0] = lax.fori_loop(0, blocks, block, jnp.zeros((8, size), jnp.float32))
-
-
-def triplet_energies(meta, own, far, tno, left, right, singles, levels, gap):
+    def with_rows(m):
+        def connect(i):
+            b0 = i * STEP
+            right_x = [right_t[0, x, :m, :].astype(jnp.bfloat16) for x in range(3)]
+            left_x = [left_t[0, x, pl.ds(b0, STEP), :] for x in range(3)]
+
+            def product(x, j):
+                row = jnp.broadcast_to(left_x[x][j : j + 1, :], (m, size)).astype(jnp.bfloat16)
+                return right_x[x] * row
+
+            for group in range(0, pairs, GROUP):
+                khatri = jnp.concatenate(
+                    [
+                        jnp.concatenate(
+                            [
+                                product(0, j), product(1, j), product(0, j + 1), product(1, j + 1),
+                                product(2, j), product(2, j + 1),
+                            ],
+                            axis=1,
+                        )
+                        for j in range(2 * group, 2 * (group + GROUP), 2)
+                    ],
+                    axis=0,
+                )
+                both = jnp.dot(khatri, weights[...], preferred_element_type=jnp.float32)
+                for k in range(GROUP):
+                    connected_s[group + k, :m, :] = both[k * m : (k + 1) * m, :]
+
+        def energies(i, total):
+            b0 = i * STEP
+            exch0_rows = exch0[pl.ds(b0, STEP), :]
+            exch2_cols = pltpu.roll(exch2[:m, :], size - b0, 1)
+            for j in range(STEP):
+                connected = connected_s[j // 2, :m, (j % 2) * size : (j % 2 + 1) * size]
+                complete = connected + singles_s[t, 1, b0 + j] * exch1[:m, :]
+                complete += columns[0, 0, :m, :] * exch0_rows[j : j + 1, :]
+                complete += exch2_cols[:, j : j + 1] * single2
+                term = connected * complete / (columns[0, 1, :m, :] + levels_s[t, b0 + j])
+                total += jnp.sum(term.reshape(m // 8, 8, size), axis=0)
+            return total
+
+        def block(i, total):
+            total = energies(i, total)
+            connect(i + 1)
+            return total
+
+        blocks = (width + STEP - 1) // STEP
+        connect(0)
+        total = lax.fori_loop(0, blocks - 1, block, jnp.zeros((8, size), jnp.float32))
+        out[0] = energies(blocks - 1, total)
+
+    needed = (width + 15) // 16 * 16
+    for m in range(size // 2, size + 1, 16):
+        pl.when(needed == m)(lambda m=m: with_rows(m))
+
+
+def triplet_energies(meta, own, far, tno, left_t, right_t, columns, singles, levels):
     trips, _, size = tno.shape
     slot = own.shape[1:]
+    pno = slot[0] * 2 // (tno.shape[1] // slot[1] + 1)
 
     def pair_spec(x):
         return pl.BlockSpec((1, *slot), lambda t, meta, *_: (meta[3 * t + x], 0, 0))
-
-    def trip_spec(shape):
-        return pl.BlockSpec((1, *shape), lambda t, *_: (t,) + (0,) * len(shape))
 
     return pl.pallas_call(
         energy_kernel,
         grid_spec=pltpu.PrefetchScalarGridSpec(
-            num_scalar_prefetch=4,
+            num_scalar_prefetch=3,
             grid=(trips,),
             in_specs=[pair_spec(x) for x in range(3)]
             + [pair_spec(x) for x in range(3)]
             + [
                 trip_spec(tno.shape[1:]),
-                trip_spec(left.shape[1:]),
-                trip_spec(right.shape[1:]),
+                trip_spec(left_t.shape[1:]),
+                trip_spec(right_t.shape[1:]),
+                trip_spec(columns.shape[1:]),
                 trip_spec(singles.shape[1:]),
-                trip_spec((1, size)),
             ],
             out_specs=trip_spec((8, size)),
             scratch_shapes=[
-                pltpu.VMEM((size, 3 * size), jnp.float32),
-                pltpu.VMEM((size, 3 * size), jnp.bfloat16),
                 pltpu.VMEM((6 * size, 2 * size), jnp.bfloat16),
                 pltpu.VMEM((size, size), jnp.float32),
                 pltpu.VMEM((size, size), jnp.float32),
                 pltpu.VMEM((size, size), jnp.float32),
-                pltpu.VMEM((size, size), jnp.float32),
-                pltpu.VMEM((size, size), jnp.float32),
-                pltpu.VMEM((size // 2, size), jnp.bfloat16),
+                pltpu.VMEM((STEP // 2, size, 2 * size), jnp.float32),
+                pltpu.VMEM((3, pno, 2 * pno), jnp.bfloat16),
             ],
         ),
         out_shape=jax.ShapeDtypeStruct((trips, 8, size), jnp.float32),
         compiler_params=pltpu.CompilerParams(dimension_semantics=("arbitrary",)),
         name="energy",
-    )(
-        meta, levels, singles, gap,
-        own, own, own, far, far, far, tno, left, right, singles, levels.reshape(trips, 1, size),
-    )
+    )(meta, levels, singles, own, own, own, far, far, far, tno, left_t, right_t, columns, singles)
+
+
+def test_entry(meta, own, far, tno, left, right, singles, levels, gap):
+    trips = tno.shape[0]
+    ready = prepare(meta[3 * trips : 4 * trips], gap, left, right, singles, levels)
+    return jnp.sum(triplet_energies(meta, own, far, tno, *ready, singles, levels), axis=(1, 2))
 
 
 def body(
@@ -253,12 +322,13 @@
     rows = jnp.concatenate([jnp.maximum(asked, 0), rep[None].astype(jnp.int32)])
     sent = send_slots(rows, pair_coeff, blocks, reps)
     got = lax.all_to_all(sent, "pair", 0, 0, tiled=True)
+    ready = prepare(tno_width, gap, int_left, int_right, singles, tno_energy)
+    got = pltpu.with_memory_space_constraint(got, pltpu.HBM)
     far = lax.ppermute(got, "rep", [(0, 1), (1, 0)])
+    far = pltpu.with_memory_space_constraint(far, pltpu.HBM)
 
     meta = jnp.concatenate([owners, tno_width, rep[None].astype(jnp.int32)])
-    partial = triplet_energies(
-        meta, got, far, tno_coeff, int_left, int_right, singles, tno_energy, gap
-    )
+    partial = triplet_energies(meta, got, far, tno_coeff, *ready, singles, tno_energy)
     energies = jnp.sum(partial, axis=(1, 2))
 
     shares = jnp.repeat(energies / 3.0, 3)

time: 192 us -> 184 us (0.958)
  blocking collectives: 74.3 us -> 82.7 us
  waiting for transfers between devices: 10.5 us -> 4.15 us
  Pallas kernels: 72.9 us -> 66.8 us
  local copies, waits for them, and re-layouts: 7.17 us -> 2.88 us
    pallas_call x1, Pallas kernels: 65.3 us -> 51.7 us  [triplet_energies(): pl.pallas_call(energy_kernel, grid_spec=pltpu.PrefetchScalarGridSpec(num_...]
    all_to_all x1, blocking collectives: 11.8 us -> 19.9 us  [body(): shares = lax.all_to_all(shares, BOTH, 0, 0, tiled=True)]
    pallas_call x0 -> x1, Pallas kernels: none -> 7.61 us  [prepare(): pl.pallas_call(prepare_kernel, grid_spec=pltpu.PrefetchScalarGridSpec(num...]
    ppermute x1, waiting for transfers between devices: 6.34 us -> 0.01 us  [body(): far = lax.ppermute(got, 'rep', [(0, 1), (1, 0)])]
    unnamed x12 -> x8, local copies, waits for them, and re-layouts: 5.67 us -> 1.38 us
  transfers between devices with their start and end apart: 2 -> 2, of which waited for: 2 -> 1; matrix products, arithmetic and copies ran while one was open for 3% -> 4% of each run, Pallas kernels for 0% -> 4%
where the time goes in v2:
time: 184 us; the launch traced here: 183 us
  blocking collectives  82.7 us (45%)
  Pallas kernels  66.8 us (36%)
  starting transfers between devices  13.9 us (8%)
  other arithmetic  11.7 us (6%)
  waiting for transfers between devices  4.15 us (2%)
  local copies, waits for them, and re-layouts  2.88 us (2%)
    all_to_all x1, blocking collectives, body(): got = lax.all_to_all(sent, 'pair', 0, 0, tiled=True)  62.8 us
    pallas_call x1, Pallas kernels, triplet_energies(): pl.pallas_call(energy_kernel, grid_spec=pltpu.PrefetchScalarGridSpec(num_...  51.7 us
    all_to_all x1, blocking collectives, body(): shares = lax.all_to_all(shares, BOTH, 0, 0, tiled=True)  19.9 us
    all_to_all x1, starting transfers between devices, body(): asked = lax.all_to_all(wanted, BOTH, 0, 0, tiled=True)  11.5 us
    pallas_call x1, Pallas kernels, prepare(): pl.pallas_call(prepare_kernel, grid_spec=pltpu.PrefetchScalarGridSpec(num...  7.61 us
    pallas_call x1, Pallas kernels, send_slots(): pl.pallas_call(lambda *refs: slots_kernel(*refs, halves=halves), grid_spe...  7.45 us
    all_to_all x1, waiting for transfers between devices, body(): asked = lax.all_to_all(wanted, BOTH, 0, 0, tiled=True)  4.15 us
  transfers between devices with their start and end apart: 2, of which 1 were waited for; matrix products, arithmetic and copies ran while one was open for 4% of the time, Pallas kernels for 4%

profile of v2, /device:TPU:1, one launch (start us, length us, event | category | flops | bytes accessed | tf_op | source)
XLA Modules:
  0.0 182.9 jit_solution(3014332456964927110)
XLA Ops:
  0.6 0.8 copy.28
  1.6 0.7 all_to_all.20
  2.4 11.5 %all-to-all-start = ((s32[128,1,1]{2,1,0:T(1,128)}), s32[128,1,1]{2,1,0:T(1,128)S(1)}, u32[]{:S(2)}, u32[]{:S(2)}) async-start(s32[128,1,1]{2,1,0:T(1,128)} %all_to_all.20), calls=%async_computation | async-start | bytes 131072 | tf_op jit(solution)/shard_map/all_to_all | solution.py:313
  13.9 0.7 iota_compare_fusion.1
  14.6 2.9 %and_select_fusion.1 = (bf16[64,64,64]{2,1,0:T(8,128)(2,1)S(1)}, bf16[64,64,64]{2,1,0:T(8,128)(2,1)S(1)}) fusion(bf16[64,64,64]{2,1,0:T(8,128)(2,1)} %param.16, pred[64,64]{1,0:T(8,128)(4,1)S(1)} %iota_compare_fusion.1, bf16[64,64,64]{2,1,0:T(8,128)(2,1)} %param.17), kind=kLoop, calls=%fused_computation.1 | loop fusion | flops 786432 | bytes 2101248 | tf_op jit(solution)/shard_map/jit(_where)/select_n | solution.py:320
  17.5 1.6 pad_maximum_fusion.refs_2_
  19.1 4.2 %all-to-all-done = s32[128,1,1]{2,1,0:T(1,128)S(1)} async-done(((s32[128,1,1]{2,1,0:T(1,128)}), s32[128,1,1]{2,1,0:T(1,128)S(1)}, u32[]{:S(2)}, u32[]{:S(2)}) %all-to-all-start) | async-done | bytes 544 | tf_op jit(solution)/shard_map/all_to_all | solution.py:313
  23.3 2.3 %reduce = s32[128]{0:T(128)S(1)} reduce(s32[128,1,1]{2,1,0:T(1,128)S(1)} %all-to-all-done, s32[]{:T(128)} %constant.36.clone.1), dimensions={1,2}, to_apply=%all_to_all.16.reduce_sub_computation | reduce | bytes 1028 | tf_op jit(solution)/shard_map/all_to_all | solution.py:313
  25.6 0.1 reshape.98
  25.8 0.1 reduce_max.9
  25.9 0.6 pad_add_fusion.1.refs_0_
  26.5 7.4 %slots.1 = bf16[64,288,128]{2,1,0:T(8,128)(2,1)} custom-call(s32[65]{0:T(128)} %pad_add_fusion.1.refs_0_, bf16[64,64,1024]{2,1,0:T(8,128)(2,1)} %refs_1_.1, bf16[64,64,128]{2,1,0:T(8,128)(2,1)} %pad_maximum_fusion.refs_2_), custom_call_target="tpu_custom_call" | custom-call | tf_op jit(solution)/shard_map/slots/pallas_call | solution.py:54
  34.0 62.8 %all_to_all.25.own0.own1.own2 = bf16[64,288,128]{2,1,0:T(8,128)(2,1)} all-to-all(bf16[64,288,128]{2,1,0:T(8,128)(2,1)} %slots.1), channel_id=1, replica_groups=mesh['pair'=64,'rep'=2] {'pair'}, dimensions={0} | all-to-all | bytes 9437184 | tf_op jit(solution)/shard_map/all_to_all | solution.py:324
  96.8 2.4 %collective-permute-start = (bf16[64,288,128]{2,1,0:T(8,128)(2,1)}, bf16[64,288,128]{2,1,0:T(8,128)(2,1)}, u32[]{:S(2)}, u32[]{:S(2)}) collective-permute-start(bf16[64,288,128]{2,1,0:T(8,128)(2,1)} %all_to_all.25.own0.own1.own2), channel_id=1, source_target_pairs={{0,1},{1,0},{2,3},{3,2},{4,5},{5,4},{6,7},{7,6},{8,9},{9,8},{10,11... | collective-permute-start | bytes 14155784 | tf_op jit(solution)/shard_map/ppermute | solution.py:327
  99.2 0.6 copy.31.singles.singles_s
  99.8 7.6 %prepare.1 = (f32[8,3,128,128]{3,2,1,0:T(8,128)}, f32[8,3,128,128]{3,2,1,0:T(8,128)}, f32[8,2,128,128]{3,2,1,0:T(8,128)}) custom-call(s32[8]{0:T(128)} %widths.1, f32[8]{0:T(128)} %gap_s.1, bf16[8,3,128,128]{3,2,1,0:T(8,128)(2,1)} %left.1, bf16[8,3,128,128]{3,2,1,0:T(8,128)(2,1)} %right.1, f32[8,3,128]{2,1,0:T(4,128)} %copy.31.singles.singles_s, ...), custom_call_target="tpu_custom_call" | custom-call | flops 201326592 | bytes 4194304 | tf_op jit(solution)/shard_map/prepare/pallas_call | solution.py:113
  107.4 0.6 pad_add_fusion.meta
  108.0 51.7 %energy.1 = f32[8,8,128]{2,1,0:T(8,128)} custom-call(s32[33]{0:T(128)} %pad_add_fusion.meta, f32[8,128]{1,0:T(8,128)} %levels_s.1, f32[8,3,128]{2,1,0:T(4,128)} %copy.31.singles.singles_s, bf16[64,288,128]{2,1,0:T(8,128)(2,1)} %all_to_all.25.own0.own1.own2, bf16[64,288,128]{2,1,0:T(8,128)(2,1)} %all_to_all.25.own0.own1.own2, ...), custom_call_target="tpu_custom_call" | custom-call | tf_op jit(solution)/shard_map/energy/pallas_call | solution.py:263
  159.7 0.9 reduce_sum.46
  160.9 0.1 all_to_all.21
  161.0 19.9 %all_to_all.26 = f32[128,1,1]{2,1,0:T(1,128)S(1)} all-to-all(f32[128,1,1]{2,1,0:T(1,128)S(1)} %all_to_all.21), channel_id=1, replica_groups=mesh['pair'=64,'rep'=2] {'pair','rep'}, dimensions={0} | all-to-all | bytes 1024 | tf_op jit(solution)/shard_map/all_to_all | solution.py:337
  181.0 1.0 reduce.1
  182.0 0.1 reshape.100
  182.3 0.6 select_reduce_fusion
  (18 shorter events, 0.7 us)
Async XLA Ops:
  2.4 20.9 %all-to-all-start = ((s32[128,1,1]{2,1,0:T(1,128)}), s32[128,1,1]{2,1,0:T(1,128)S(1)}, u32[]{:S(2)}, u32[]{:S(2)}) async-start(s32[128,1,1]{2,1,0:T(1,128)} %all_to_all.20), calls=%async_computation | async-start | bytes 131072 | tf_op jit(solution)/shard_map/all_to_all | solution.py:313
  33.9 65.2 %copy-start = (f32[8,3,128]{2,0,1:T(8,128)S(1)}, f32[8,3,128]{2,0,1:T(8,128)}, u32[]{:S(2)}) copy-start(f32[8,3,128]{2,0,1:T(8,128)} %param.21) | copy-start | bytes 36868
  34.0 73.4 %copy-start.1 = (s32[8]{0:T(128)S(1)}, s32[8]{0:T(128)}, u32[]{:S(2)}) copy-start(s32[8]{0:T(128)} %widths.1) | copy-start | bytes 100
  96.8 11.2 %collective-permute-start = (bf16[64,288,128]{2,1,0:T(8,128)(2,1)}, bf16[64,288,128]{2,1,0:T(8,128)(2,1)}, u32[]{:S(2)}, u32[]{:S(2)}) collective-permute-start(bf16[64,288,128]{2,1,0:T(8,128)(2,1)} %all_to_all.25.own0.own1.own2), channel_id=1, source_target_pairs={{0,1},{1,0},{2,3},{3,2},{4,5},{5,4},{6,7},{7,6},{8,9},{9,8},{10,11... | collective-permute-start | bytes 14155784 | tf_op jit(solution)/shard_map/ppermute | solution.py:327
  160.6 22.3 %copy-start.2 = (f32[8]{0:T(128)}, f32[8]{0:T(128)S(1)}, u32[]{:S(2)}) copy-start(f32[8]{0:T(128)S(1)} %reduce_sum.46) | copy-start | bytes 100

commit v3 on v2

--- a/solution.py
+++ b/solution.py
@@ -8,24 +8,35 @@
 BOTH = ("pair", "rep")
 
 
-def slots_kernel(rows, coeff, blocks, out, buf, got, put, *, halves):
-    slots, slot_rows, lanes = buf.shape
+def slots_kernel(
+    rep_s, asked, coeff, blocks, out, buf, asked_v, asked_s, got, put, fetched, *, halves
+):
+    slots, _, lanes = out.shape
     pno = coeff.shape[1]
     dom_part = coeff.shape[2] // halves
     pieces = dom_part // lanes
     pair_rows = pno // halves
-    rep = rows[slots]
+    rep = rep_s[0]
+    row = lax.broadcasted_iota(jnp.int32, asked.shape, 0)
+    col = lax.broadcasted_iota(jnp.int32, asked.shape, 1)
+    asked_v[...] = jnp.sum(jnp.where(row == col, asked[...], 0), axis=0, keepdims=True)
+    fetch = pltpu.make_async_copy(asked_v, asked_s, fetched)
+    fetch.start()
+    fetch.wait()
 
     def start(s, _):
-        row = rows[s]
+        wanted = asked_s[0, halves * s]
+        for h in range(1, halves):
+            wanted = jnp.maximum(wanted, asked_s[0, halves * s + h])
+        pair = jnp.maximum(wanted - 1, 0)
         for piece in range(pieces):
             pltpu.make_async_copy(
-                coeff.at[row, :, pl.ds(rep * dom_part + piece * lanes, lanes)],
+                coeff.at[pair, :, pl.ds(rep * dom_part + piece * lanes, lanes)],
                 buf.at[s, pl.ds(piece * pno, pno), :],
                 got.at[s],
             ).start()
         pltpu.make_async_copy(
-            blocks.at[row, pl.ds(rep * pair_rows, pair_rows), :],
+            blocks.at[pair, pl.ds(rep * pair_rows, pair_rows), :],
             buf.at[s, pl.ds(pieces * pno, pair_rows), :],
             got.at[s],
         ).start()
@@ -45,8 +56,8 @@
     lax.fori_loop(0, slots, finish, 0)
 
 
-def send_slots(rows, coeff, blocks, halves):
-    slots = rows.shape[0] - 1
+def send_slots(rep, asked, coeff, blocks, halves):
+    slots = asked.shape[0] // halves
     _, pno, domain = coeff.shape
     lanes = blocks.shape[2]
     slot_rows = pno * (domain // halves // lanes) + pno // halves
@@ -56,17 +67,24 @@
         grid_spec=pltpu.PrefetchScalarGridSpec(
             num_scalar_prefetch=1,
             grid=(),
-            in_specs=[pl.BlockSpec(memory_space=pl.ANY), pl.BlockSpec(memory_space=pl.ANY)],
+            in_specs=[
+                pl.BlockSpec(memory_space=pltpu.VMEM),
+                pl.BlockSpec(memory_space=pl.ANY),
+                pl.BlockSpec(memory_space=pl.ANY),
+            ],
             out_specs=pl.BlockSpec(memory_space=pl.ANY),
             scratch_shapes=[
                 pltpu.VMEM(shape, jnp.bfloat16),
+                pltpu.VMEM((1, asked.shape[0]), jnp.int32),
+                pltpu.SMEM((1, asked.shape[0]), jnp.int32),
                 pltpu.SemaphoreType.DMA((slots,)),
                 pltpu.SemaphoreType.DMA((slots,)),
+                pltpu.SemaphoreType.DMA(()),
             ],
         ),
         out_shape=jax.ShapeDtypeStruct(shape, jnp.bfloat16),
         name="slots",
-    )(rows, coeff, blocks)
+    )(rep, asked, coeff, blocks)
 
 
 def dot_nt(x, y):
@@ -144,7 +162,7 @@
     meta, levels_s, singles_s,
     own0, own1, own2, far0, far1, far2, tno, left_t, right_t, columns, singles,
     out,
-    weights, exch0, exch1, exch2, connected_s, ix,
+    weights, exch0, exch1, exch2, connected_s, outer_s, ix,
 ):
     t = pl.program_id(0)
     trips = levels_s.shape[0]
@@ -197,7 +215,7 @@
     single2 = singles[0, 2:3, :]
 
     def with_rows(m):
-        def connect(i):
+        def connect(side, i):
             b0 = i * STEP
             right_x = [right_t[0, x, :m, :].astype(jnp.bfloat16) for x in range(3)]
             left_x = [left_t[0, x, pl.ds(b0, STEP), :] for x in range(3)]
@@ -222,30 +240,36 @@
                 )
                 both = jnp.dot(khatri, weights[...], preferred_element_type=jnp.float32)
                 for k in range(GROUP):
-                    connected_s[group + k, :m, :] = both[k * m : (k + 1) * m, :]
-
-        def energies(i, total):
+                    connected_s[side, group + k, :m, :] = both[k * m : (k + 1) * m, :]
+            exch2_cols = pltpu.roll(exch2[:m, :], size - b0, 1)
+            for j in range(STEP):
+                outer_s[side, j, :m, :] = jnp.broadcast_to(exch2_cols[:, j : j + 1], (m, size))
+
+        def energies(side, i, total):
             b0 = i * STEP
             exch0_rows = exch0[pl.ds(b0, STEP), :]
-            exch2_cols = pltpu.roll(exch2[:m, :], size - b0, 1)
             for j in range(STEP):
-                connected = connected_s[j // 2, :m, (j % 2) * size : (j % 2 + 1) * size]
+                connected = connected_s[side, j // 2, :m, (j % 2) * size : (j % 2 + 1) * size]
                 complete = connected + singles_s[t, 1, b0 + j] * exch1[:m, :]
                 complete += columns[0, 0, :m, :] * exch0_rows[j : j + 1, :]
-                complete += exch2_cols[:, j : j + 1] * single2
+                complete += outer_s[side, j, :m, :] * single2
                 term = connected * complete / (columns[0, 1, :m, :] + levels_s[t, b0 + j])
                 total += jnp.sum(term.reshape(m // 8, 8, size), axis=0)
             return total
 
         def block(i, total):
-            total = energies(i, total)
-            connect(i + 1)
+            total = energies(0, 2 * i, total)
+            connect(1, 2 * i + 1)
+            total = energies(1, 2 * i + 1, total)
+            connect(0, 2 * i + 2)
             return total
 
-        blocks = (width + STEP - 1) // STEP
-        connect(0)
-        total = lax.fori_loop(0, blocks - 1, block, jnp.zeros((8, size), jnp.float32))
-        out[0] = energies(blocks - 1, total)
+        last = m // (2 * STEP) - 1
+        connect(0, 0)
+        total = lax.fori_loop(0, last, block, jnp.zeros((8, size), jnp.float32))
+        total = energies(0, 2 * last, total)
+        connect(1, 2 * last + 1)
+        out[0] = energies(1, 2 * last + 1, total)
 
     needed = (width + 15) // 16 * 16
     for m in range(size // 2, size + 1, 16):
@@ -280,7 +304,8 @@
                 pltpu.VMEM((size, size), jnp.float32),
                 pltpu.VMEM((size, size), jnp.float32),
                 pltpu.VMEM((size, size), jnp.float32),
-                pltpu.VMEM((STEP // 2, size, 2 * size), jnp.float32),
+                pltpu.VMEM((2, STEP // 2, size, 2 * size), jnp.float32),
+                pltpu.VMEM((2, STEP, size, size), jnp.float32),
                 pltpu.VMEM((3, pno, 2 * pno), jnp.bfloat16),
             ],
         ),
@@ -306,12 +331,12 @@
     rep = lax.axis_index("rep")
     references = triplet_pairs.reshape(-1)
     owners = references // pair_dev
-    at_owner = owners[None, :] == jnp.arange(owners_n, dtype=jnp.int32)[:, None]
-
-    wanted = jnp.sum(jnp.where(at_owner, references % pair_dev + 1, 0), axis=1)
-    wanted = jnp.broadcast_to(wanted[:, None], (owners_n, reps)).reshape(-1, 1)
-    asked = lax.all_to_all(wanted, BOTH, 0, 0, tiled=True)
-    asked = jnp.max(asked.reshape(owners_n, reps), axis=1) - 1
+    peers = owners_n * reps
+    wide = 128
+    peer = lax.broadcasted_iota(jnp.int32, (1, peers, wide), 1) // reps
+    at_peer = owners[:, None, None] == peer
+    wanted = jnp.sum(jnp.where(at_peer, (references % pair_dev + 1)[:, None, None], 0), axis=0)
+    asked = lax.all_to_all(wanted[:, None, :], BOTH, 0, 0, tiled=True).reshape(peers, wide)
 
     kept = jnp.arange(pno, dtype=jnp.int32)[None, :] < pair_width[:, None]
     kept = kept[:, :, None] & kept[:, None, :]
@@ -319,8 +344,7 @@
     blocks = jnp.concatenate(
         [jnp.where(kept, pair_amps, zero), jnp.where(kept, pair_exch, zero)], axis=2
     )
-    rows = jnp.concatenate([jnp.maximum(asked, 0), rep[None].astype(jnp.int32)])
-    sent = send_slots(rows, pair_coeff, blocks, reps)
+    sent = send_slots(rep[None].astype(jnp.int32), asked, pair_coeff, blocks, reps)
     got = lax.all_to_all(sent, "pair", 0, 0, tiled=True)
     ready = prepare(tno_width, gap, int_left, int_right, singles, tno_energy)
     got = pltpu.with_memory_space_constraint(got, pltpu.HBM)
@@ -332,12 +356,10 @@
     energies = jnp.sum(partial, axis=(1, 2))
 
     shares = jnp.repeat(energies / 3.0, 3)
-    shares = jnp.sum(jnp.where(at_owner, shares[None, :], 0.0), axis=1)
-    shares = jnp.broadcast_to(shares[:, None], (owners_n, reps)).reshape(-1, 1)
-    shares = lax.all_to_all(shares, BOTH, 0, 0, tiled=True)
-    shares = jnp.sum(shares.reshape(owners_n, reps), axis=1)
-    here = asked[None, :] == jnp.arange(pair_dev, dtype=jnp.int32)[:, None]
-    pair_energy = jnp.sum(jnp.where(here, shares[None, :], 0.0), axis=1)
+    shares = jnp.sum(jnp.where(at_peer, shares[:, None, None], 0.0), axis=0)
+    shares = lax.all_to_all(shares[:, None, :], BOTH, 0, 0, tiled=True).reshape(peers, wide)
+    here = asked == lax.broadcasted_iota(jnp.int32, (peers, wide), 1) + 1
+    pair_energy = jnp.sum(jnp.where(here, shares, 0.0), axis=0)[:pair_dev]
     return (energies, pair_energy)
 
 

time: 184 us -> 180 us (0.978)
  blocking collectives: 82.7 us -> 62.5 us
  starting transfers between devices: 13.9 us -> 28.6 us
  waiting for transfers between devices: 4.15 us -> 13.5 us
  Pallas kernels: 66.8 us -> 61.9 us
  other arithmetic: 11.7 us -> 9.06 us
    all_to_all x1 -> x0, blocking collectives: 19.9 us -> none  [body(): shares = lax.all_to_all(shares, BOTH, 0, 0, tiled=True)]
    all_to_all x1 -> x2, starting transfers between devices: 11.5 us -> 26.1 us  [the longest x1 14.6 us: body(): lax.all_to_all(shares[:, None, :], BOTH, 0, 0, tiled=True)]
    all_to_all x1 -> x2, waiting for transfers between devices: 4.15 us -> 13.5 us  [the longest x1 9.37 us: body(): lax.all_to_all(shares[:, None, :], BOTH, 0, 0, tiled=True)]
    pallas_call x1, Pallas kernels: 51.7 us -> 46.4 us  [triplet_energies(): pl.pallas_call(energy_kernel, grid_spec=pltpu.PrefetchScalarGridSpec(num_...]
    all_to_all x2 -> x0, other arithmetic: 3.38 us -> none  [the longest x1 2.35 us: body(): asked = lax.all_to_all(wanted, BOTH, 0, 0, tiled=True)]
  transfers between devices with their start and end apart: 2 -> 3, of which waited for: 1 -> 2; matrix products, arithmetic and copies ran while one was open for 4% -> 4% of each run, Pallas kernels for 4% -> 4%
where the time goes in v3:
time: 180 us; the launch traced here: 179 us
  blocking collectives  62.5 us (35%)
  Pallas kernels  61.9 us (34%)
  starting transfers between devices  28.6 us (16%)
  waiting for transfers between devices  13.5 us (8%)
  other arithmetic  9.06 us (5%)
  local copies, waits for them, and re-layouts  2.23 us (1%)
    all_to_all x1, blocking collectives, body(): got = lax.all_to_all(sent, 'pair', 0, 0, tiled=True)  62.5 us
    pallas_call x1, Pallas kernels, triplet_energies(): pl.pallas_call(energy_kernel, grid_spec=pltpu.PrefetchScalarGridSpec(num_...  46.4 us
    all_to_all x1, starting transfers between devices, body(): lax.all_to_all(shares[:, None, :], BOTH, 0, 0, tiled=True)  14.6 us
    all_to_all x1, starting transfers between devices, body(): lax.all_to_all(wanted[:, None, :], BOTH, 0, 0, tiled=True)  11.5 us
    all_to_all x1, waiting for transfers between devices, body(): lax.all_to_all(shares[:, None, :], BOTH, 0, 0, tiled=True)  9.37 us
    pallas_call x1, Pallas kernels, send_slots(): pl.pallas_call(lambda *refs: slots_kernel(*refs, halves=halves), grid_spe...  7.87 us
    pallas_call x1, Pallas kernels, prepare(): pl.pallas_call(prepare_kernel, grid_spec=pltpu.PrefetchScalarGridSpec(num...  7.64 us
    all_to_all x1, waiting for transfers between devices, body(): lax.all_to_all(wanted[:, None, :], BOTH, 0, 0, tiled=True)  4.17 us
  transfers between devices with their start and end apart: 3, of which 2 were waited for; matrix products, arithmetic and copies ran while one was open for 4% of the time, Pallas kernels for 4%

profile of v3, /device:TPU:1, one launch (start us, length us, event | category | flops | bytes accessed | tf_op | source)
XLA Modules:
  0.0 178.6 jit_solution(5088044522109473035)
XLA Ops:
  0.7 0.8 copy.26
  1.4 0.1 reshape.138
  1.5 0.1 broadcast_select_fusion
  1.6 0.8 fusion
  2.5 11.5 %all-to-all-start = ((s32[128,1,128]{2,1,0:T(1,128)}), s32[128,1,128]{2,1,0:T(1,128)S(1)}, u32[]{:S(2)}, u32[]{:S(2)}) async-start(s32[128,1,128]{2,1,0:T(1,128)} %bitcast.2), calls=%async_computation | async-start | bytes 131072 | tf_op jit(solution)/shard_map/all_to_all | solution.py:339
  14.0 0.7 iota_compare_fusion
  14.7 2.9 %and_select_fusion.1 = (bf16[64,64,64]{2,1,0:T(8,128)(2,1)S(1)}, bf16[64,64,64]{2,1,0:T(8,128)(2,1)S(1)}) fusion(bf16[64,64,64]{2,1,0:T(8,128)(2,1)} %param.16, pred[64,64]{1,0:T(8,128)(4,1)S(1)} %iota_compare_fusion, bf16[64,64,64]{2,1,0:T(8,128)(2,1)} %param.17), kind=kLoop, calls=%fused_computation.1 | loop fusion | flops 786432 | bytes 2101248 | tf_op jit(solution)/shard_map/jit(_where)/select_n | solution.py:345
  17.6 1.6 pad_maximum_fusion.refs_3_
  19.2 4.2 %all-to-all-done = s32[128,1,128]{2,1,0:T(1,128)S(1)} async-done(((s32[128,1,128]{2,1,0:T(1,128)}), s32[128,1,128]{2,1,0:T(1,128)S(1)}, u32[]{:S(2)}, u32[]{:S(2)}) %all-to-all-start) | async-done | bytes 65568 | tf_op jit(solution)/shard_map/all_to_all | solution.py:339
  23.4 0.6 copy-done
  24.0 7.9 %slots.1 = bf16[64,288,128]{2,1,0:T(8,128)(2,1)} custom-call(s32[1]{0:T(128)} %bitcast.refs_0_, s32[128,128]{1,0:T(8,128)} %bitcast.11, bf16[64,64,1024]{2,1,0:T(8,128)(2,1)} %refs_2_.1, bf16[64,64,128]{2,1,0:T(8,128)(2,1)} %pad_maximum_fusion.refs_3_), custom_call_target="tpu_custom_call" | custom-call | tf_op jit(solution)/shard_map/slots/pallas_call | solution.py:65
  31.9 62.5 %all_to_all.15.own0.own1.own2 = bf16[64,288,128]{2,1,0:T(8,128)(2,1)} all-to-all(bf16[64,288,128]{2,1,0:T(8,128)(2,1)} %slots.1), channel_id=1, replica_groups=mesh['pair'=64,'rep'=2] {'pair'}, dimensions={0} | all-to-all | bytes 9437184 | tf_op jit(solution)/shard_map/all_to_all | solution.py:348
  94.4 2.5 %collective-permute-start = (bf16[64,288,128]{2,1,0:T(8,128)(2,1)}, bf16[64,288,128]{2,1,0:T(8,128)(2,1)}, u32[]{:S(2)}, u32[]{:S(2)}) collective-permute-start(bf16[64,288,128]{2,1,0:T(8,128)(2,1)} %all_to_all.15.own0.own1.own2), channel_id=1, source_target_pairs={{0,1},{1,0},{2,3},{3,2},{4,5},{5,4},{6,7},{7,6},{8,9},{9,8},{10,11... | collective-permute-start | bytes 14155784 | tf_op jit(solution)/shard_map/ppermute | solution.py:351
  96.9 0.6 copy.29.singles.singles_s
  97.5 7.6 %prepare.1 = (f32[8,3,128,128]{3,2,1,0:T(8,128)}, f32[8,3,128,128]{3,2,1,0:T(8,128)}, f32[8,2,128,128]{3,2,1,0:T(8,128)}) custom-call(s32[8]{0:T(128)} %widths.1, f32[8]{0:T(128)} %gap_s.1, bf16[8,3,128,128]{3,2,1,0:T(8,128)(2,1)} %left.1, bf16[8,3,128,128]{3,2,1,0:T(8,128)(2,1)} %right.1, f32[8,3,128]{2,1,0:T(4,128)} %copy.29.singles.singles_s, ...), custom_call_target="tpu_custom_call" | custom-call | flops 201326592 | bytes 4194304 | tf_op jit(solution)/shard_map/prepare/pallas_call | solution.py:131
  105.2 0.6 pad_add_fusion.meta
  105.8 46.4 %energy.1 = f32[8,8,128]{2,1,0:T(8,128)} custom-call(s32[33]{0:T(128)} %pad_add_fusion.meta, f32[8,128]{1,0:T(8,128)} %levels_s.1, f32[8,3,128]{2,1,0:T(4,128)} %copy.29.singles.singles_s, bf16[64,288,128]{2,1,0:T(8,128)(2,1)} %all_to_all.15.own0.own1.own2, bf16[64,288,128]{2,1,0:T(8,128)(2,1)} %all_to_all.15.own0.own1.own2, ...), custom_call_target="tpu_custom_call" | custom-call | tf_op jit(solution)/shard_map/energy/pallas_call | solution.py:287
  152.1 0.9 reduce_sum.37
  153.0 0.1 broadcast_in_dim.59
  153.1 0.1 broadcast_in_dim.60
  153.2 0.8 fusion.1
  154.0 14.6 %all-to-all-start.2 = ((f32[128,1,128]{2,1,0:T(1,128)}), f32[128,1,128]{2,1,0:T(1,128)S(1)}, u32[]{:S(2)}, u32[]{:S(2)}) async-start(f32[128,1,128]{2,1,0:T(1,128)} %bitcast.6), calls=%async_computation.2 | async-start | bytes 131072 | tf_op jit(solution)/shard_map/all_to_all | solution.py:360
  168.6 9.4 %all-to-all-done.2 = f32[128,1,128]{2,1,0:T(1,128)S(1)} async-done(((f32[128,1,128]{2,1,0:T(1,128)}), f32[128,1,128]{2,1,0:T(1,128)S(1)}, u32[]{:S(2)}, u32[]{:S(2)}) %all-to-all-start.2) | async-done | bytes 65568 | tf_op jit(solution)/shard_map/all_to_all | solution.py:360
  178.0 0.5 select_reduce_fusion
  (15 shorter events, 0.1 us)
Async XLA Ops:
  2.5 20.9 %all-to-all-start = ((s32[128,1,128]{2,1,0:T(1,128)}), s32[128,1,128]{2,1,0:T(1,128)S(1)}, u32[]{:S(2)}, u32[]{:S(2)}) async-start(s32[128,1,128]{2,1,0:T(1,128)} %bitcast.2), calls=%async_computation | async-start | bytes 131072 | tf_op jit(solution)/shard_map/all_to_all | solution.py:339
  23.4 0.6 copy-start
  31.9 65.1 %copy-start.2 = (f32[8,3,128]{2,0,1:T(8,128)S(1)}, f32[8,3,128]{2,0,1:T(8,128)}, u32[]{:S(2)}) copy-start(f32[8,3,128]{2,0,1:T(8,128)} %param.21) | copy-start | bytes 36868
  94.4 10.8 %copy-start.3 = (s32[8]{0:T(128)S(1)}, s32[8]{0:T(128)}, u32[]{:S(2)}) copy-start(s32[8]{0:T(128)} %widths.1) | copy-start | bytes 100
  94.4 11.4 %collective-permute-start = (bf16[64,288,128]{2,1,0:T(8,128)(2,1)}, bf16[64,288,128]{2,1,0:T(8,128)(2,1)}, u32[]{:S(2)}, u32[]{:S(2)}) collective-permute-start(bf16[64,288,128]{2,1,0:T(8,128)(2,1)} %all_to_all.15.own0.own1.own2), channel_id=1, source_target_pairs={{0,1},{1,0},{2,3},{3,2},{4,5},{5,4},{6,7},{7,6},{8,9},{9,8},{10,11... | collective-permute-start | bytes 14155784 | tf_op jit(solution)/shard_map/ppermute | solution.py:351
  105.8 72.3 %copy-start.1 = (s32[128,1,128]{2,1,0:T(1,128)S(1)}, s32[128,1,128]{2,1,0:T(1,128)}, u32[]{:S(2)}) copy-start(s32[128,1,128]{2,1,0:T(1,128)} %copy-done) | copy-start | bytes 196612
  153.0 25.5 %copy-start.4 = (f32[8]{0:T(128)}, f32[8]{0:T(128)S(1)}, u32[]{:S(2)}) copy-start(f32[8]{0:T(128)S(1)} %reduce_sum.37) | copy-start | bytes 100
  154.0 24.0 %all-to-all-start.2 = ((f32[128,1,128]{2,1,0:T(1,128)}), f32[128,1,128]{2,1,0:T(1,128)S(1)}, u32[]{:S(2)}, u32[]{:S(2)}) async-start(f32[128,1,128]{2,1,0:T(1,128)} %bitcast.6), calls=%async_computation.2 | async-start | bytes 131072 | tf_op jit(solution)/shard_map/all_to_all | solution.py:360

commit v4 on v3

--- a/solution.py
+++ b/solution.py
@@ -241,9 +241,8 @@
                 both = jnp.dot(khatri, weights[...], preferred_element_type=jnp.float32)
                 for k in range(GROUP):
                     connected_s[side, group + k, :m, :] = both[k * m : (k + 1) * m, :]
-            exch2_cols = pltpu.roll(exch2[:m, :], size - b0, 1)
             for j in range(STEP):
-                outer_s[side, j, :m, :] = jnp.broadcast_to(exch2_cols[:, j : j + 1], (m, size))
+                outer_s[side, j, :m, :] = jnp.broadcast_to(exch2[:m, b0 + j : b0 + j + 1], (m, size))
 
         def energies(side, i, total):
             b0 = i * STEP
@@ -257,19 +256,14 @@
                 total += jnp.sum(term.reshape(m // 8, 8, size), axis=0)
             return total
 
-        def block(i, total):
-            total = energies(0, 2 * i, total)
-            connect(1, 2 * i + 1)
-            total = energies(1, 2 * i + 1, total)
-            connect(0, 2 * i + 2)
-            return total
-
-        last = m // (2 * STEP) - 1
+        steps = m // STEP
+        total = jnp.zeros((8, size), jnp.float32)
         connect(0, 0)
-        total = lax.fori_loop(0, last, block, jnp.zeros((8, size), jnp.float32))
-        total = energies(0, 2 * last, total)
-        connect(1, 2 * last + 1)
-        out[0] = energies(1, 2 * last + 1, total)
+        for i in range(steps):
+            total = energies(i % 2, i, total)
+            if i + 1 < steps:
+                connect((i + 1) % 2, i + 1)
+        out[0] = total
 
     needed = (width + 15) // 16 * 16
     for m in range(size // 2, size + 1, 16):

time: 180 us -> 167 us (0.928)
  Pallas kernels: 61.9 us -> 52.3 us
  starting transfers between devices: 28.6 us -> 25.2 us
    pallas_call x1, Pallas kernels: 46.4 us -> 36.8 us  [triplet_energies(): pl.pallas_call(energy_kernel, grid_spec=pltpu.PrefetchScalarGridSpec(num_...]
    all_to_all x1, starting transfers between devices: 14.6 us -> 11.1 us  [body(): lax.all_to_all(shares[:, None, :], BOTH, 0, 0, tiled=True)]
  transfers between devices with their start and end apart: 3 -> 3, of which waited for: 2 -> 2; matrix products, arithmetic and copies ran while one was open for 4% -> 4% of each run, Pallas kernels for 4% -> 5%
where the time goes in v4:
time: 167 us; the launch traced here: 166 us
  blocking collectives  62.6 us (37%)
  Pallas kernels  52.3 us (31%)
  starting transfers between devices  25.2 us (15%)
  waiting for transfers between devices  13.5 us (8%)
  other arithmetic  9.06 us (5%)
  local copies, waits for them, and re-layouts  2.23 us (1%)
    all_to_all x1, blocking collectives, body(): got = lax.all_to_all(sent, 'pair', 0, 0, tiled=True)  62.6 us
    pallas_call x1, Pallas kernels, triplet_energies(): pl.pallas_call(energy_kernel, grid_spec=pltpu.PrefetchScalarGridSpec(num_...  36.8 us
    all_to_all x1, starting transfers between devices, body(): lax.all_to_all(wanted[:, None, :], BOTH, 0, 0, tiled=True)  11.5 us
    all_to_all x1, starting transfers between devices, body(): lax.all_to_all(shares[:, None, :], BOTH, 0, 0, tiled=True)  11.1 us
    all_to_all x1, waiting for transfers between devices, body(): lax.all_to_all(shares[:, None, :], BOTH, 0, 0, tiled=True)  9.37 us
    pallas_call x1, Pallas kernels, send_slots(): pl.pallas_call(lambda *refs: slots_kernel(*refs, halves=halves), grid_spe...  7.81 us
    pallas_call x1, Pallas kernels, prepare(): pl.pallas_call(prepare_kernel, grid_spec=pltpu.PrefetchScalarGridSpec(num...  7.64 us
    all_to_all x1, waiting for transfers between devices, body(): lax.all_to_all(wanted[:, None, :], BOTH, 0, 0, tiled=True)  4.17 us
  transfers between devices with their start and end apart: 3, of which 2 were waited for; matrix products, arithmetic and copies ran while one was open for 4% of the time, Pallas kernels for 5%

profile of v4, /device:TPU:1, one launch (start us, length us, event | category | flops | bytes accessed | tf_op | source)
XLA Modules:
  0.0 165.6 jit_solution(4246167078549855106)
XLA Ops:
  0.7 0.8 copy.26
  1.4 0.1 reshape.138
  1.5 0.1 broadcast_select_fusion
  1.6 0.8 fusion
  2.5 11.5 %all-to-all-start = ((s32[128,1,128]{2,1,0:T(1,128)}), s32[128,1,128]{2,1,0:T(1,128)S(1)}, u32[]{:S(2)}, u32[]{:S(2)}) async-start(s32[128,1,128]{2,1,0:T(1,128)} %bitcast.2), calls=%async_computation | async-start | bytes 131072 | tf_op jit(solution)/shard_map/all_to_all | solution.py:333
  14.0 0.7 iota_compare_fusion
  14.7 2.9 %and_select_fusion.1 = (bf16[64,64,64]{2,1,0:T(8,128)(2,1)S(1)}, bf16[64,64,64]{2,1,0:T(8,128)(2,1)S(1)}) fusion(bf16[64,64,64]{2,1,0:T(8,128)(2,1)} %param.16, pred[64,64]{1,0:T(8,128)(4,1)S(1)} %iota_compare_fusion, bf16[64,64,64]{2,1,0:T(8,128)(2,1)} %param.17), kind=kLoop, calls=%fused_computation.1 | loop fusion | flops 786432 | bytes 2101248 | tf_op jit(solution)/shard_map/jit(_where)/select_n | solution.py:339
  17.6 1.6 pad_maximum_fusion.refs_3_
  19.2 4.2 %all-to-all-done = s32[128,1,128]{2,1,0:T(1,128)S(1)} async-done(((s32[128,1,128]{2,1,0:T(1,128)}), s32[128,1,128]{2,1,0:T(1,128)S(1)}, u32[]{:S(2)}, u32[]{:S(2)}) %all-to-all-start) | async-done | bytes 65568 | tf_op jit(solution)/shard_map/all_to_all | solution.py:333
  23.4 0.6 copy-done
  24.0 7.8 %slots.1 = bf16[64,288,128]{2,1,0:T(8,128)(2,1)} custom-call(s32[1]{0:T(128)} %bitcast.refs_0_, s32[128,128]{1,0:T(8,128)} %bitcast.11, bf16[64,64,1024]{2,1,0:T(8,128)(2,1)} %refs_2_.1, bf16[64,64,128]{2,1,0:T(8,128)(2,1)} %pad_maximum_fusion.refs_3_), custom_call_target="tpu_custom_call" | custom-call | tf_op jit(solution)/shard_map/slots/pallas_call | solution.py:65
  31.8 62.6 %all_to_all.15.own0.own1.own2 = bf16[64,288,128]{2,1,0:T(8,128)(2,1)} all-to-all(bf16[64,288,128]{2,1,0:T(8,128)(2,1)} %slots.1), channel_id=1, replica_groups=mesh['pair'=64,'rep'=2] {'pair'}, dimensions={0} | all-to-all | bytes 9437184 | tf_op jit(solution)/shard_map/all_to_all | solution.py:342
  94.4 2.6 %collective-permute-start = (bf16[64,288,128]{2,1,0:T(8,128)(2,1)}, bf16[64,288,128]{2,1,0:T(8,128)(2,1)}, u32[]{:S(2)}, u32[]{:S(2)}) collective-permute-start(bf16[64,288,128]{2,1,0:T(8,128)(2,1)} %all_to_all.15.own0.own1.own2), channel_id=1, source_target_pairs={{0,1},{1,0},{2,3},{3,2},{4,5},{5,4},{6,7},{7,6},{8,9},{9,8},{10,11... | collective-permute-start | bytes 14155784 | tf_op jit(solution)/shard_map/ppermute | solution.py:345
  97.0 0.6 copy.29.singles.singles_s
  97.6 7.6 %prepare.1 = (f32[8,3,128,128]{3,2,1,0:T(8,128)}, f32[8,3,128,128]{3,2,1,0:T(8,128)}, f32[8,2,128,128]{3,2,1,0:T(8,128)}) custom-call(s32[8]{0:T(128)} %widths.1, f32[8]{0:T(128)} %gap_s.1, bf16[8,3,128,128]{3,2,1,0:T(8,128)(2,1)} %left.1, bf16[8,3,128,128]{3,2,1,0:T(8,128)(2,1)} %right.1, f32[8,3,128]{2,1,0:T(4,128)} %copy.29.singles.singles_s, ...), custom_call_target="tpu_custom_call" | custom-call | flops 201326592 | bytes 4194304 | tf_op jit(solution)/shard_map/prepare/pallas_call | solution.py:131
  105.2 0.6 pad_add_fusion.meta
  105.8 36.8 %energy.1 = f32[8,8,128]{2,1,0:T(8,128)} custom-call(s32[33]{0:T(128)} %pad_add_fusion.meta, f32[8,128]{1,0:T(8,128)} %levels_s.1, f32[8,3,128]{2,1,0:T(4,128)} %copy.29.singles.singles_s, bf16[64,288,128]{2,1,0:T(8,128)(2,1)} %all_to_all.15.own0.own1.own2, bf16[64,288,128]{2,1,0:T(8,128)(2,1)} %all_to_all.15.own0.own1.own2, ...), custom_call_target="tpu_custom_call" | custom-call | tf_op jit(solution)/shard_map/energy/pallas_call | solution.py:281
  142.7 0.9 reduce_sum.37
  143.6 0.1 broadcast_in_dim.59
  143.6 0.1 broadcast_in_dim.60
  143.7 0.8 fusion.1
  144.6 11.1 %all-to-all-start.2 = ((f32[128,1,128]{2,1,0:T(1,128)}), f32[128,1,128]{2,1,0:T(1,128)S(1)}, u32[]{:S(2)}, u32[]{:S(2)}) async-start(f32[128,1,128]{2,1,0:T(1,128)} %bitcast.6), calls=%async_computation.2 | async-start | bytes 131072 | tf_op jit(solution)/shard_map/all_to_all | solution.py:354
  155.7 9.4 %all-to-all-done.2 = f32[128,1,128]{2,1,0:T(1,128)S(1)} async-done(((f32[128,1,128]{2,1,0:T(1,128)}), f32[128,1,128]{2,1,0:T(1,128)S(1)}, u32[]{:S(2)}, u32[]{:S(2)}) %all-to-all-start.2) | async-done | bytes 65568 | tf_op jit(solution)/shard_map/all_to_all | solution.py:354
  165.1 0.5 select_reduce_fusion
  (15 shorter events, 0.1 us)
Async XLA Ops:
  2.5 20.9 %all-to-all-start = ((s32[128,1,128]{2,1,0:T(1,128)}), s32[128,1,128]{2,1,0:T(1,128)S(1)}, u32[]{:S(2)}, u32[]{:S(2)}) async-start(s32[128,1,128]{2,1,0:T(1,128)} %bitcast.2), calls=%async_computation | async-start | bytes 131072 | tf_op jit(solution)/shard_map/all_to_all | solution.py:333
  23.4 0.6 copy-start
  31.8 65.2 %copy-start.2 = (f32[8,3,128]{2,0,1:T(8,128)S(1)}, f32[8,3,128]{2,0,1:T(8,128)}, u32[]{:S(2)}) copy-start(f32[8,3,128]{2,0,1:T(8,128)} %param.21) | copy-start | bytes 36868
  94.4 10.8 %copy-start.3 = (s32[8]{0:T(128)S(1)}, s32[8]{0:T(128)}, u32[]{:S(2)}) copy-start(s32[8]{0:T(128)} %widths.1) | copy-start | bytes 100
  94.4 11.4 %collective-permute-start = (bf16[64,288,128]{2,1,0:T(8,128)(2,1)}, bf16[64,288,128]{2,1,0:T(8,128)(2,1)}, u32[]{:S(2)}, u32[]{:S(2)}) collective-permute-start(bf16[64,288,128]{2,1,0:T(8,128)(2,1)} %all_to_all.15.own0.own1.own2), channel_id=1, source_target_pairs={{0,1},{1,0},{2,3},{3,2},{4,5},{5,4},{6,7},{7,6},{8,9},{9,8},{10,11... | collective-permute-start | bytes 14155784 | tf_op jit(solution)/shard_map/ppermute | solution.py:345
  105.8 59.2 %copy-start.1 = (s32[128,1,128]{2,1,0:T(1,128)S(1)}, s32[128,1,128]{2,1,0:T(1,128)}, u32[]{:S(2)}) copy-start(s32[128,1,128]{2,1,0:T(1,128)} %copy-done) | copy-start | bytes 196612
  143.6 22.1 %copy-start.4 = (f32[8]{0:T(128)}, f32[8]{0:T(128)S(1)}, u32[]{:S(2)}) copy-start(f32[8]{0:T(128)S(1)} %reduce_sum.37) | copy-start | bytes 100
  144.6 20.5 %all-to-all-start.2 = ((f32[128,1,128]{2,1,0:T(1,128)}), f32[128,1,128]{2,1,0:T(1,128)S(1)}, u32[]{:S(2)}, u32[]{:S(2)}) async-start(f32[128,1,128]{2,1,0:T(1,128)} %bitcast.6), calls=%async_computation.2 | async-start | bytes 131072 | tf_op jit(solution)/shard_map/all_to_all | solution.py:354

commit v5 on v4

--- a/solution.py
+++ b/solution.py
@@ -162,11 +162,13 @@
     meta, levels_s, singles_s,
     own0, own1, own2, far0, far1, far2, tno, left_t, right_t, columns, singles,
     out,
-    weights, exch0, exch1, exch2, connected_s, outer_s, ix,
+    weights, exch, next_weights, next_exch, connected_s, outer_s, ix,
 ):
-    t = pl.program_id(0)
+    step = pl.program_id(0)
     trips = levels_s.shape[0]
+    t = jnp.maximum(step - 1, 0)
     width = meta[3 * trips + t]
+    next_width = meta[3 * trips + jnp.minimum(step, trips - 1)]
     rep = meta[4 * trips]
     own = (own0, own1, own2)
     far = (far0, far1, far2)
@@ -185,34 +187,32 @@
             rows.append(jnp.concatenate(cols, axis=1))
         return jnp.concatenate(rows, axis=0)
 
-    inter = jnp.dot(
-        stacked(own), tno[0, pl.ds(rep * half_dom, half_dom), :], preferred_element_type=jnp.float32
-    )
-    inter += jnp.dot(
-        stacked(far),
-        tno[0, pl.ds((1 - rep) * half_dom, half_dom), :],
-        preferred_element_type=jnp.float32,
-    )
-    lane = lax.broadcasted_iota(jnp.int32, inter.shape, 1)
-    inter = jnp.where(lane < width, inter, 0.0).astype(jnp.bfloat16)
-
-    @pl.when(t == 0)
-    def _():
-        weights[...] = jnp.zeros(weights.shape, weights.dtype)
-
-    exch = (exch0, exch1, exch2)
+    def project():
+        inter = jnp.dot(
+            stacked(own),
+            tno[0, pl.ds(rep * half_dom, half_dom), :],
+            preferred_element_type=jnp.float32,
+        )
+        inter += jnp.dot(
+            stacked(far),
+            tno[0, pl.ds((1 - rep) * half_dom, half_dom), :],
+            preferred_element_type=jnp.float32,
+        )
+        lane = lax.broadcasted_iota(jnp.int32, inter.shape, 1)
+        inter = jnp.where(lane < next_width, inter, 0.0).astype(jnp.bfloat16)
+        for x in range(3):
+            mine = own[x][0, pieces * pno : pieces * pno + part, :]
+            other = far[x][0, pieces * pno : pieces * pno + part, :]
+            ix[x, pl.ds(rep * part, part), :] = mine
+            ix[x, pl.ds((1 - rep) * part, part), :] = other
+        for x in range(3):
+            inter_x = inter[x * pno : (x + 1) * pno, :]
+            halfway = dot_tn(inter_x, ix[x]).astype(jnp.bfloat16)
+            next_weights[x] = dot_tt(inter_x, halfway[:, :pno]).astype(jnp.bfloat16)
+            next_exch[x] = dot_tt(inter_x, halfway[:, pno:])
+
+    single2 = singles[0, 2:3, :]
     spots = ((0, 256), (128, 384), (512, 640))
-    for x in range(3):
-        ix[x, pl.ds(rep * part, part), :] = own[x][0, pieces * pno : pieces * pno + part, :]
-        ix[x, pl.ds((1 - rep) * part, part), :] = far[x][0, pieces * pno : pieces * pno + part, :]
-    for x in range(3):
-        inter_x = inter[x * pno : (x + 1) * pno, :]
-        halfway = dot_tn(inter_x, ix[x]).astype(jnp.bfloat16)
-        amps = dot_tt(inter_x, halfway[:, :pno]).astype(jnp.bfloat16)
-        exch[x][...] = dot_tt(inter_x, halfway[:, pno:])
-        weights[spots[x][0] : spots[x][0] + size, :size] = amps
-        weights[spots[x][1] : spots[x][1] + size, size:] = amps
-    single2 = singles[0, 2:3, :]
 
     def with_rows(m):
         def connect(side, i):
@@ -242,14 +242,15 @@
                 for k in range(GROUP):
                     connected_s[side, group + k, :m, :] = both[k * m : (k + 1) * m, :]
             for j in range(STEP):
-                outer_s[side, j, :m, :] = jnp.broadcast_to(exch2[:m, b0 + j : b0 + j + 1], (m, size))
+                column = exch[2, :m, b0 + j : b0 + j + 1]
+                outer_s[side, j, :m, :] = jnp.broadcast_to(column, (m, size))
 
         def energies(side, i, total):
             b0 = i * STEP
-            exch0_rows = exch0[pl.ds(b0, STEP), :]
+            exch0_rows = exch[0, pl.ds(b0, STEP), :]
             for j in range(STEP):
                 connected = connected_s[side, j // 2, :m, (j % 2) * size : (j % 2 + 1) * size]
-                complete = connected + singles_s[t, 1, b0 + j] * exch1[:m, :]
+                complete = connected + singles_s[t, 1, b0 + j] * exch[1, :m, :]
                 complete += columns[0, 0, :m, :] * exch0_rows[j : j + 1, :]
                 complete += outer_s[side, j, :m, :] * single2
                 term = connected * complete / (columns[0, 1, :m, :] + levels_s[t, b0 + j])
@@ -263,11 +264,25 @@
             total = energies(i % 2, i, total)
             if i + 1 < steps:
                 connect((i + 1) % 2, i + 1)
+            if i == 1:
+                project()
         out[0] = total
 
-    needed = (width + 15) // 16 * 16
-    for m in range(size // 2, size + 1, 16):
-        pl.when(needed == m)(lambda m=m: with_rows(m))
+    @pl.when(step == 0)
+    def _():
+        weights[...] = jnp.zeros(weights.shape, weights.dtype)
+        project()
+
+    @pl.when(step > 0)
+    def _():
+        for x in range(3):
+            amps = next_weights[x]
+            weights[spots[x][0] : spots[x][0] + size, :size] = amps
+            weights[spots[x][1] : spots[x][1] + size, size:] = amps
+            exch[x] = next_exch[x]
+        needed = (width + 15) // 16 * 16
+        for m in range(size // 2, size + 1, 16):
+            pl.when(needed == m)(lambda m=m: with_rows(m))
 
 
 def triplet_energies(meta, own, far, tno, left_t, right_t, columns, singles, levels):
@@ -275,29 +290,37 @@
     slot = own.shape[1:]
     pno = slot[0] * 2 // (tno.shape[1] // slot[1] + 1)
 
+    def ahead(s):
+        return jnp.minimum(s, trips - 1)
+
+    def behind_spec(shape):
+        return pl.BlockSpec(
+            (1, *shape), lambda s, *_: (jnp.maximum(s - 1, 0),) + (0,) * len(shape)
+        )
+
     def pair_spec(x):
-        return pl.BlockSpec((1, *slot), lambda t, meta, *_: (meta[3 * t + x], 0, 0))
+        return pl.BlockSpec((1, *slot), lambda s, meta, *_: (meta[3 * ahead(s) + x], 0, 0))
 
     return pl.pallas_call(
         energy_kernel,
         grid_spec=pltpu.PrefetchScalarGridSpec(
             num_scalar_prefetch=3,
-            grid=(trips,),
+            grid=(trips + 1,),
             in_specs=[pair_spec(x) for x in range(3)]
             + [pair_spec(x) for x in range(3)]
             + [
-                trip_spec(tno.shape[1:]),
-                trip_spec(left_t.shape[1:]),
-                trip_spec(right_t.shape[1:]),
-                trip_spec(columns.shape[1:]),
-                trip_spec(singles.shape[1:]),
-            ],
-            out_specs=trip_spec((8, size)),
+                pl.BlockSpec((1, *tno.shape[1:]), lambda s, *_: (ahead(s), 0, 0)),
+                behind_spec(left_t.shape[1:]),
+                behind_spec(right_t.shape[1:]),
+                behind_spec(columns.shape[1:]),
+                behind_spec(singles.shape[1:]),
+            ],
+            out_specs=behind_spec((8, size)),
             scratch_shapes=[
                 pltpu.VMEM((6 * size, 2 * size), jnp.bfloat16),
-                pltpu.VMEM((size, size), jnp.float32),
-                pltpu.VMEM((size, size), jnp.float32),
-                pltpu.VMEM((size, size), jnp.float32),
+                pltpu.VMEM((3, size, size), jnp.float32),
+                pltpu.VMEM((3, size, size), jnp.bfloat16),
+                pltpu.VMEM((3, size, size), jnp.float32),
                 pltpu.VMEM((2, STEP // 2, size, 2 * size), jnp.float32),
                 pltpu.VMEM((2, STEP, size, size), jnp.float32),
                 pltpu.VMEM((3, pno, 2 * pno), jnp.bfloat16),
@@ -341,6 +364,7 @@
     sent = send_slots(rep[None].astype(jnp.int32), asked, pair_coeff, blocks, reps)
     got = lax.all_to_all(sent, "pair", 0, 0, tiled=True)
     ready = prepare(tno_width, gap, int_left, int_right, singles, tno_energy)
+    got, ready = lax.optimization_barrier((got, ready))
     got = pltpu.with_memory_space_constraint(got, pltpu.HBM)
     far = lax.ppermute(got, "rep", [(0, 1), (1, 0)])
     far = pltpu.with_memory_space_constraint(far, pltpu.HBM)

time: 167 us -> 174 us (1.042)
  blocking collectives: 62.6 us -> 0 us
  waiting for transfers between devices: 13.5 us -> 71.2 us
  starting transfers between devices: 25.2 us -> 36.4 us
    all_to_all x1 -> x0, blocking collectives: 62.6 us -> none  [body(): got = lax.all_to_all(sent, 'pair', 0, 0, tiled=True)]
    all_to_all x0 -> x1, waiting for transfers between devices: none -> 50.4 us  [body(): got = lax.all_to_all(sent, 'pair', 0, 0, tiled=True)]
    ppermute x1, waiting for transfers between devices: 0.01 us -> 7.29 us  [body(): far = lax.ppermute(got, 'rep', [(0, 1), (1, 0)])]
    all_to_all x0 -> x1, starting transfers between devices: none -> 6.34 us  [body(): got = lax.all_to_all(sent, 'pair', 0, 0, tiled=True)]
    all_to_all x1, starting transfers between devices: 11.1 us -> 17.1 us  [body(): lax.all_to_all(shares[:, None, :], BOTH, 0, 0, tiled=True)]
  transfers between devices with their start and end apart: 3 -> 4, of which waited for: 2 -> 4; matrix products, arithmetic and copies ran while one was open for 4% -> 4% of each run, Pallas kernels for 5% -> 4%
where the time goes in v5:
time: 174 us; the launch traced here: 172 us
  waiting for transfers between devices  71.2 us (41%)
  Pallas kernels  52.2 us (30%)
  starting transfers between devices  36.4 us (21%)
  other arithmetic  9.06 us (5%)
  local copies, waits for them, and re-layouts  2.24 us (1%)
    all_to_all x1, waiting for transfers between devices, body(): got = lax.all_to_all(sent, 'pair', 0, 0, tiled=True)  50.4 us
    pallas_call x1, Pallas kernels, triplet_energies(): pl.pallas_call(energy_kernel, grid_spec=pltpu.PrefetchScalarGridSpec(num_...  36.7 us
    all_to_all x1, starting transfers between devices, body(): lax.all_to_all(shares[:, None, :], BOTH, 0, 0, tiled=True)  17.1 us
    all_to_all x1, starting transfers between devices, body(): lax.all_to_all(wanted[:, None, :], BOTH, 0, 0, tiled=True)  11.5 us
    all_to_all x1, waiting for transfers between devices, body(): lax.all_to_all(shares[:, None, :], BOTH, 0, 0, tiled=True)  9.34 us
    pallas_call x1, Pallas kernels, send_slots(): pl.pallas_call(lambda *refs: slots_kernel(*refs, halves=halves), grid_spe...  7.93 us
    pallas_call x1, Pallas kernels, prepare(): pl.pallas_call(prepare_kernel, grid_spec=pltpu.PrefetchScalarGridSpec(num...  7.62 us
    ppermute x1, waiting for transfers between devices, body(): far = lax.ppermute(got, 'rep', [(0, 1), (1, 0)])  7.29 us
  transfers between devices with their start and end apart: 4, of which 4 were waited for; matrix products, arithmetic and copies ran while one was open for 4% of the time, Pallas kernels for 4%

profile of v5, /device:TPU:1, one launch (start us, length us, event | category | flops | bytes accessed | tf_op | source)
XLA Modules:
  0.0 171.9 jit_solution(8939434819146157536)
XLA Ops:
  0.7 0.8 copy.26
  1.5 0.1 broadcast_select_fusion
  1.6 0.8 fusion
  2.5 11.5 %all-to-all-start = ((s32[128,1,128]{2,1,0:T(1,128)}), s32[128,1,128]{2,1,0:T(1,128)S(1)}, u32[]{:S(2)}, u32[]{:S(2)}) async-start(s32[128,1,128]{2,1,0:T(1,128)} %bitcast.2), calls=%async_computation | async-start | bytes 131072 | tf_op jit(solution)/shard_map/all_to_all | solution.py:356
  14.0 0.7 iota_compare_fusion
  14.7 2.9 %and_select_fusion.1 = (bf16[64,64,64]{2,1,0:T(8,128)(2,1)S(1)}, bf16[64,64,64]{2,1,0:T(8,128)(2,1)S(1)}) fusion(bf16[64,64,64]{2,1,0:T(8,128)(2,1)} %param.16, pred[64,64]{1,0:T(8,128)(4,1)S(1)} %iota_compare_fusion, bf16[64,64,64]{2,1,0:T(8,128)(2,1)} %param.17), kind=kLoop, calls=%fused_computation.1 | loop fusion | flops 786432 | bytes 2101248 | tf_op jit(solution)/shard_map/jit(_where)/select_n | solution.py:362
  17.6 1.6 pad_maximum_fusion.refs_3_
  19.2 4.2 %all-to-all-done = s32[128,1,128]{2,1,0:T(1,128)S(1)} async-done(((s32[128,1,128]{2,1,0:T(1,128)}), s32[128,1,128]{2,1,0:T(1,128)S(1)}, u32[]{:S(2)}, u32[]{:S(2)}) %all-to-all-start) | async-done | bytes 65568 | tf_op jit(solution)/shard_map/all_to_all | solution.py:356
  23.4 0.6 copy-done
  24.0 7.9 %slots.1 = bf16[64,288,128]{2,1,0:T(8,128)(2,1)} custom-call(s32[1]{0:T(128)} %bitcast.refs_0_, s32[128,128]{1,0:T(8,128)} %bitcast.11, bf16[64,64,1024]{2,1,0:T(8,128)(2,1)} %refs_2_.1, bf16[64,64,128]{2,1,0:T(8,128)(2,1)} %pad_maximum_fusion.refs_3_), custom_call_target="tpu_custom_call" | custom-call | tf_op jit(solution)/shard_map/slots/pallas_call | solution.py:65
  31.9 6.3 %all-to-all-start.1 = ((bf16[64,288,128]{2,1,0:T(8,128)(2,1)}), bf16[64,288,128]{2,1,0:T(8,128)(2,1)}, u32[]{:S(2)}, u32[]{:S(2)}) async-start(bf16[64,288,128]{2,1,0:T(8,128)(2,1)} %slots.1), calls=%async_computation.1 | async-start | bytes 9437184 | tf_op jit(solution)/shard_map/all_to_all | solution.py:365
  38.3 0.6 copy.29.singles.singles_s
  38.9 7.6 %prepare.1 = (f32[8,3,128,128]{3,2,1,0:T(8,128)}, f32[8,3,128,128]{3,2,1,0:T(8,128)}, f32[8,2,128,128]{3,2,1,0:T(8,128)}) custom-call(s32[8]{0:T(128)} %widths.1, f32[8]{0:T(128)} %gap_s.1, bf16[8,3,128,128]{3,2,1,0:T(8,128)(2,1)} %left.1, bf16[8,3,128,128]{3,2,1,0:T(8,128)(2,1)} %right.1, f32[8,3,128]{2,1,0:T(4,128)} %copy.29.singles.singles_s, ...), custom_call_target="tpu_custom_call" | custom-call | flops 201326592 | bytes 4194304 | tf_op jit(solution)/shard_map/prepare/pallas_call | solution.py:131
  46.5 50.4 %all-to-all-done.1.own0.own1.own2 = bf16[64,288,128]{2,1,0:T(8,128)(2,1)} async-done(((bf16[64,288,128]{2,1,0:T(8,128)(2,1)}), bf16[64,288,128]{2,1,0:T(8,128)(2,1)}, u32[]{:S(2)}, u32[]{:S(2)}) %all-to-all-start.1) | async-done | bytes 4718624 | tf_op jit(solution)/shard_map/all_to_all | solution.py:365
  96.9 1.5 collective-permute-start
  98.4 0.6 pad_add_fusion.meta
  99.0 7.3 %collective-permute-done.far0.far1.far2 = bf16[64,288,128]{2,1,0:T(8,128)(2,1)} collective-permute-done((bf16[64,288,128]{2,1,0:T(8,128)(2,1)}, bf16[64,288,128]{2,1,0:T(8,128)(2,1)}, u32[]{:S(2)}, u32[]{:S(2)}) %collective-permute-start) | collective-permute-done | bytes 4718624 | tf_op jit(solution)/shard_map/ppermute | solution.py:369
  106.3 36.7 %energy.1 = f32[8,8,128]{2,1,0:T(8,128)} custom-call(s32[33]{0:T(128)} %pad_add_fusion.meta, f32[8,128]{1,0:T(8,128)} %levels_s.1, f32[8,3,128]{2,1,0:T(4,128)} %copy.29.singles.singles_s, bf16[64,288,128]{2,1,0:T(8,128)(2,1)} %all-to-all-done.1.own0.own1.own2, bf16[64,288,128]{2,1,0:T(8,128)(2,1)} %all-to-all-done.1.own0.own1.own2, ...), custom_call_target="tpu_custom_call" | custom-call | tf_op jit(solution)/shard_map/energy/pallas_call | solution.py:304
  143.0 0.9 reduce_sum.37
  143.9 0.1 broadcast_in_dim.60
  144.0 0.8 fusion.1
  144.9 17.1 %all-to-all-start.2 = ((f32[128,1,128]{2,1,0:T(1,128)}), f32[128,1,128]{2,1,0:T(1,128)S(1)}, u32[]{:S(2)}, u32[]{:S(2)}) async-start(f32[128,1,128]{2,1,0:T(1,128)} %bitcast.6), calls=%async_computation.2 | async-start | bytes 131072 | tf_op jit(solution)/shard_map/all_to_all | solution.py:378
  162.0 9.3 %all-to-all-done.2 = f32[128,1,128]{2,1,0:T(1,128)S(1)} async-done(((f32[128,1,128]{2,1,0:T(1,128)}), f32[128,1,128]{2,1,0:T(1,128)S(1)}, u32[]{:S(2)}, u32[]{:S(2)}) %all-to-all-start.2) | async-done | bytes 65568 | tf_op jit(solution)/shard_map/all_to_all | solution.py:378
  171.4 0.5 select_reduce_fusion
  (16 shorter events, 0.2 us)
Async XLA Ops:
  2.5 20.9 %all-to-all-start = ((s32[128,1,128]{2,1,0:T(1,128)}), s32[128,1,128]{2,1,0:T(1,128)S(1)}, u32[]{:S(2)}, u32[]{:S(2)}) async-start(s32[128,1,128]{2,1,0:T(1,128)} %bitcast.2), calls=%async_computation | async-start | bytes 131072 | tf_op jit(solution)/shard_map/all_to_all | solution.py:356
  23.4 0.6 copy-start
  31.9 6.4 %copy-start.2 = (f32[8,3,128]{2,0,1:T(8,128)S(1)}, f32[8,3,128]{2,0,1:T(8,128)}, u32[]{:S(2)}) copy-start(f32[8,3,128]{2,0,1:T(8,128)} %param.21) | copy-start | bytes 36868
  31.9 65.0 %all-to-all-start.1 = ((bf16[64,288,128]{2,1,0:T(8,128)(2,1)}), bf16[64,288,128]{2,1,0:T(8,128)(2,1)}, u32[]{:S(2)}, u32[]{:S(2)}) async-start(bf16[64,288,128]{2,1,0:T(8,128)(2,1)} %slots.1), calls=%async_computation.1 | async-start | bytes 9437184 | tf_op jit(solution)/shard_map/all_to_all | solution.py:365
  38.3 60.1 %copy-start.3 = (s32[8]{0:T(128)S(1)}, s32[8]{0:T(128)}, u32[]{:S(2)}) copy-start(s32[8]{0:T(128)} %widths.1) | copy-start | bytes 100
  96.9 9.4 %collective-permute-start = (bf16[64,288,128]{2,1,0:T(8,128)(2,1)}, bf16[64,288,128]{2,1,0:T(8,128)(2,1)}, u32[]{:S(2)}, u32[]{:S(2)}) collective-permute-start(bf16[64,288,128]{2,1,0:T(8,128)(2,1)} %all-to-all-done.1.own0.own1.own2), channel_id=1, source_target_pairs={{0,1},{1,0},{2,3},{3,2},{4,5},{5,4},{6,7},{7,6},{8,9},{9,8},{10,11... | collective-permute-start | bytes 14155784 | tf_op jit(solution)/shard_map/ppermute | solution.py:369
  99.0 72.4 %copy-start.1 = (s32[128,1,128]{2,1,0:T(1,128)S(1)}, s32[128,1,128]{2,1,0:T(1,128)}, u32[]{:S(2)}) copy-start(s32[128,1,128]{2,1,0:T(1,128)} %copy-done) | copy-start | bytes 196612
  143.8 28.1 %copy-start.4 = (f32[8]{0:T(128)}, f32[8]{0:T(128)S(1)}, u32[]{:S(2)}) copy-start(f32[8]{0:T(128)S(1)} %reduce_sum.37) | copy-start | bytes 100
  144.9 26.5 %all-to-all-start.2 = ((f32[128,1,128]{2,1,0:T(1,128)}), f32[128,1,128]{2,1,0:T(1,128)S(1)}, u32[]{:S(2)}, u32[]{:S(2)}) async-start(f32[128,1,128]{2,1,0:T(1,128)} %bitcast.6), calls=%async_computation.2 | async-start | bytes 131072 | tf_op jit(solution)/shard_map/all_to_all | solution.py:378

commit v6 on v5

--- a/solution.py
+++ b/solution.py
@@ -364,7 +364,6 @@
     sent = send_slots(rep[None].astype(jnp.int32), asked, pair_coeff, blocks, reps)
     got = lax.all_to_all(sent, "pair", 0, 0, tiled=True)
     ready = prepare(tno_width, gap, int_left, int_right, singles, tno_energy)
-    got, ready = lax.optimization_barrier((got, ready))
     got = pltpu.with_memory_space_constraint(got, pltpu.HBM)
     far = lax.ppermute(got, "rep", [(0, 1), (1, 0)])
     far = pltpu.with_memory_space_constraint(far, pltpu.HBM)

time: 174 us -> 167 us (0.960)
  blocking collectives: 0 us -> 63.3 us
  waiting for transfers between devices: 71.2 us -> 13.5 us
  starting transfers between devices: 36.4 us -> 22.6 us
    all_to_all x0 -> x1, blocking collectives: none -> 63.3 us  [body(): got = lax.all_to_all(sent, 'pair', 0, 0, tiled=True)]
    all_to_all x1 -> x0, waiting for transfers between devices: 50.4 us -> none  [body(): got = lax.all_to_all(sent, 'pair', 0, 0, tiled=True)]
    all_to_all x1, starting transfers between devices: 17.1 us -> 8.21 us  [body(): lax.all_to_all(shares[:, None, :], BOTH, 0, 0, tiled=True)]
    ppermute x1, waiting for transfers between devices: 7.29 us -> 0.01 us  [body(): far = lax.ppermute(got, 'rep', [(0, 1), (1, 0)])]
    all_to_all x1 -> x0, starting transfers between devices: 6.34 us -> none  [body(): got = lax.all_to_all(sent, 'pair', 0, 0, tiled=True)]
  transfers between devices with their start and end apart: 4 -> 3, of which waited for: 4 -> 2; matrix products, arithmetic and copies ran while one was open for 4% -> 4% of each run, Pallas kernels for 4% -> 5%
where the time goes in v6:
time: 167 us; the launch traced here: 164 us
  blocking collectives  63.3 us (38%)
  Pallas kernels  53 us (32%)
  starting transfers between devices  22.6 us (14%)
  waiting for transfers between devices  13.5 us (8%)
  other arithmetic  9.06 us (5%)
  local copies, waits for them, and re-layouts  2.23 us (1%)
    all_to_all x1, blocking collectives, body(): got = lax.all_to_all(sent, 'pair', 0, 0, tiled=True)  63.3 us
    pallas_call x1, Pallas kernels, triplet_energies(): pl.pallas_call(energy_kernel, grid_spec=pltpu.PrefetchScalarGridSpec(num_...  37.8 us
    all_to_all x1, starting transfers between devices, body(): lax.all_to_all(wanted[:, None, :], BOTH, 0, 0, tiled=True)  11.5 us
    all_to_all x1, waiting for transfers between devices, body(): lax.all_to_all(shares[:, None, :], BOTH, 0, 0, tiled=True)  9.37 us
    all_to_all x1, starting transfers between devices, body(): lax.all_to_all(shares[:, None, :], BOTH, 0, 0, tiled=True)  8.21 us
    pallas_call x1, Pallas kernels, prepare(): pl.pallas_call(prepare_kernel, grid_spec=pltpu.PrefetchScalarGridSpec(num...  7.64 us
    pallas_call x1, Pallas kernels, send_slots(): pl.pallas_call(lambda *refs: slots_kernel(*refs, halves=halves), grid_spe...  7.54 us
    all_to_all x1, waiting for transfers between devices, body(): lax.all_to_all(wanted[:, None, :], BOTH, 0, 0, tiled=True)  4.17 us
  transfers between devices with their start and end apart: 3, of which 2 were waited for; matrix products, arithmetic and copies ran while one was open for 4% of the time, Pallas kernels for 5%

profile of v6, /device:TPU:1, one launch (start us, length us, event | category | flops | bytes accessed | tf_op | source)
XLA Modules:
  0.0 164.4 jit_solution(13541834202539099721)
XLA Ops:
  0.7 0.8 copy.26
  1.4 0.1 reshape.138
  1.5 0.1 broadcast_select_fusion
  1.6 0.8 fusion
  2.5 11.5 %all-to-all-start = ((s32[128,1,128]{2,1,0:T(1,128)}), s32[128,1,128]{2,1,0:T(1,128)S(1)}, u32[]{:S(2)}, u32[]{:S(2)}) async-start(s32[128,1,128]{2,1,0:T(1,128)} %bitcast.2), calls=%async_computation | async-start | bytes 131072 | tf_op jit(solution)/shard_map/all_to_all | solution.py:356
  14.0 0.7 iota_compare_fusion
  14.7 2.9 %and_select_fusion.1 = (bf16[64,64,64]{2,1,0:T(8,128)(2,1)S(1)}, bf16[64,64,64]{2,1,0:T(8,128)(2,1)S(1)}) fusion(bf16[64,64,64]{2,1,0:T(8,128)(2,1)} %param.16, pred[64,64]{1,0:T(8,128)(4,1)S(1)} %iota_compare_fusion, bf16[64,64,64]{2,1,0:T(8,128)(2,1)} %param.17), kind=kLoop, calls=%fused_computation.1 | loop fusion | flops 786432 | bytes 2101248 | tf_op jit(solution)/shard_map/jit(_where)/select_n | solution.py:362
  17.6 1.6 pad_maximum_fusion.refs_3_
  19.2 4.2 %all-to-all-done = s32[128,1,128]{2,1,0:T(1,128)S(1)} async-done(((s32[128,1,128]{2,1,0:T(1,128)}), s32[128,1,128]{2,1,0:T(1,128)S(1)}, u32[]{:S(2)}, u32[]{:S(2)}) %all-to-all-start) | async-done | bytes 65568 | tf_op jit(solution)/shard_map/all_to_all | solution.py:356
  23.4 0.6 copy-done
  24.0 7.5 %slots.1 = bf16[64,288,128]{2,1,0:T(8,128)(2,1)} custom-call(s32[1]{0:T(128)} %bitcast.refs_0_, s32[128,128]{1,0:T(8,128)} %bitcast.11, bf16[64,64,1024]{2,1,0:T(8,128)(2,1)} %refs_2_.1, bf16[64,64,128]{2,1,0:T(8,128)(2,1)} %pad_maximum_fusion.refs_3_), custom_call_target="tpu_custom_call" | custom-call | tf_op jit(solution)/shard_map/slots/pallas_call | solution.py:65
  31.5 63.3 %all_to_all.15.own0.own1.own2 = bf16[64,288,128]{2,1,0:T(8,128)(2,1)} all-to-all(bf16[64,288,128]{2,1,0:T(8,128)(2,1)} %slots.1), channel_id=1, replica_groups=mesh['pair'=64,'rep'=2] {'pair'}, dimensions={0} | all-to-all | bytes 9437184 | tf_op jit(solution)/shard_map/all_to_all | solution.py:365
  94.8 2.9 %collective-permute-start = (bf16[64,288,128]{2,1,0:T(8,128)(2,1)}, bf16[64,288,128]{2,1,0:T(8,128)(2,1)}, u32[]{:S(2)}, u32[]{:S(2)}) collective-permute-start(bf16[64,288,128]{2,1,0:T(8,128)(2,1)} %all_to_all.15.own0.own1.own2), channel_id=1, source_target_pairs={{0,1},{1,0},{2,3},{3,2},{4,5},{5,4},{6,7},{7,6},{8,9},{9,8},{10,11... | collective-permute-start | bytes 14155784 | tf_op jit(solution)/shard_map/ppermute | solution.py:368
  97.7 0.6 copy.29.singles.singles_s
  98.3 7.6 %prepare.1 = (f32[8,3,128,128]{3,2,1,0:T(8,128)}, f32[8,3,128,128]{3,2,1,0:T(8,128)}, f32[8,2,128,128]{3,2,1,0:T(8,128)}) custom-call(s32[8]{0:T(128)} %widths.1, f32[8]{0:T(128)} %gap_s.1, bf16[8,3,128,128]{3,2,1,0:T(8,128)(2,1)} %left.1, bf16[8,3,128,128]{3,2,1,0:T(8,128)(2,1)} %right.1, f32[8,3,128]{2,1,0:T(4,128)} %copy.29.singles.singles_s, ...), custom_call_target="tpu_custom_call" | custom-call | flops 201326592 | bytes 4194304 | tf_op jit(solution)/shard_map/prepare/pallas_call | solution.py:131
  106.0 0.6 pad_add_fusion.meta
  106.6 37.8 %energy.1 = f32[8,8,128]{2,1,0:T(8,128)} custom-call(s32[33]{0:T(128)} %pad_add_fusion.meta, f32[8,128]{1,0:T(8,128)} %levels_s.1, f32[8,3,128]{2,1,0:T(4,128)} %copy.29.singles.singles_s, bf16[64,288,128]{2,1,0:T(8,128)(2,1)} %all_to_all.15.own0.own1.own2, bf16[64,288,128]{2,1,0:T(8,128)(2,1)} %all_to_all.15.own0.own1.own2, ...), custom_call_target="tpu_custom_call" | custom-call | tf_op jit(solution)/shard_map/energy/pallas_call | solution.py:304
  144.4 0.9 reduce_sum.37
  145.3 0.1 broadcast_in_dim.59
  145.3 0.1 broadcast_in_dim.60
  145.4 0.8 fusion.1
  146.3 8.2 %all-to-all-start.2 = ((f32[128,1,128]{2,1,0:T(1,128)}), f32[128,1,128]{2,1,0:T(1,128)S(1)}, u32[]{:S(2)}, u32[]{:S(2)}) async-start(f32[128,1,128]{2,1,0:T(1,128)} %bitcast.6), calls=%async_computation.2 | async-start | bytes 131072 | tf_op jit(solution)/shard_map/all_to_all | solution.py:377
  154.5 9.4 %all-to-all-done.2 = f32[128,1,128]{2,1,0:T(1,128)S(1)} async-done(((f32[128,1,128]{2,1,0:T(1,128)}), f32[128,1,128]{2,1,0:T(1,128)S(1)}, u32[]{:S(2)}, u32[]{:S(2)}) %all-to-all-start.2) | async-done | bytes 65568 | tf_op jit(solution)/shard_map/all_to_all | solution.py:377
  163.9 0.5 select_reduce_fusion
  (15 shorter events, 0.1 us)
Async XLA Ops:
  2.5 20.9 %all-to-all-start = ((s32[128,1,128]{2,1,0:T(1,128)}), s32[128,1,128]{2,1,0:T(1,128)S(1)}, u32[]{:S(2)}, u32[]{:S(2)}) async-start(s32[128,1,128]{2,1,0:T(1,128)} %bitcast.2), calls=%async_computation | async-start | bytes 131072 | tf_op jit(solution)/shard_map/all_to_all | solution.py:356
  23.4 0.6 copy-start
  31.5 66.2 %copy-start.2 = (f32[8,3,128]{2,0,1:T(8,128)S(1)}, f32[8,3,128]{2,0,1:T(8,128)}, u32[]{:S(2)}) copy-start(f32[8,3,128]{2,0,1:T(8,128)} %param.21) | copy-start | bytes 36868
  94.8 11.1 %copy-start.3 = (s32[8]{0:T(128)S(1)}, s32[8]{0:T(128)}, u32[]{:S(2)}) copy-start(s32[8]{0:T(128)} %widths.1) | copy-start | bytes 100
  94.8 11.7 %collective-permute-start = (bf16[64,288,128]{2,1,0:T(8,128)(2,1)}, bf16[64,288,128]{2,1,0:T(8,128)(2,1)}, u32[]{:S(2)}, u32[]{:S(2)}) collective-permute-start(bf16[64,288,128]{2,1,0:T(8,128)(2,1)} %all_to_all.15.own0.own1.own2), channel_id=1, source_target_pairs={{0,1},{1,0},{2,3},{3,2},{4,5},{5,4},{6,7},{7,6},{8,9},{9,8},{10,11... | collective-permute-start | bytes 14155784 | tf_op jit(solution)/shard_map/ppermute | solution.py:368
  106.6 57.3 %copy-start.1 = (s32[128,1,128]{2,1,0:T(1,128)S(1)}, s32[128,1,128]{2,1,0:T(1,128)}, u32[]{:S(2)}) copy-start(s32[128,1,128]{2,1,0:T(1,128)} %copy-done) | copy-start | bytes 196612
  145.3 19.1 %copy-start.4 = (f32[8]{0:T(128)}, f32[8]{0:T(128)S(1)}, u32[]{:S(2)}) copy-start(f32[8]{0:T(128)S(1)} %reduce_sum.37) | copy-start | bytes 100
  146.3 17.6 %all-to-all-start.2 = ((f32[128,1,128]{2,1,0:T(1,128)}), f32[128,1,128]{2,1,0:T(1,128)S(1)}, u32[]{:S(2)}, u32[]{:S(2)}) async-start(f32[128,1,128]{2,1,0:T(1,128)} %bitcast.6), calls=%async_computation.2 | async-start | bytes 131072 | tf_op jit(solution)/shard_map/all_to_all | solution.py:377
